TPU v7x, 32 devices: a whole 2x2x4 slice. The times are simulated.
32 devices in a mesh: ga: 2 (over y), gx: 4 (over z), gy: 2 (over x), col: 2 (over core).
Axes of the slice: x: 2, y: 2, z: 4, core: 2. Of those that a mesh axis runs over, the one named last changes fastest.
Arguments:
- pair_rep: bfloat16 [2, 160, 160, 128], P('ga', 'gx', 'gy'), parts along dimension 0, may hold values from -6 to 6
- pair_mask: int32 [2, 160, 160], P('ga', 'gx', 'gy'), parts along dimension 0, may hold values 0 or 1
- amax_history: float32 [2, 128], P(None, 'col'), may hold values from 0.3 to 3
- in_gain: float32 [128], replicated, may hold values from 0.5 to 1.5
- in_bias: float32 [128], replicated, may hold values from -3 to 3
- proj_weight: bfloat16 [128, 4, 128], P(None, None, 'col'), may hold values from -0.5 to 0.5
- gate_weight: bfloat16 [128, 128], P(None, 'col'), may hold values from -0.5 to 0.5
- out_gain: float32 [128], replicated, may hold values from 0.5 to 1.5
- out_bias: float32 [128], replicated, may hold values from -3 to 3
- out_weight: bfloat16 [128, 128], P(None, 'col'), may hold values from -0.5 to 0.5
Outputs:
- update: bfloat16 [2, 160, 160, 128], P('ga', 'gx', 'gy', 'col'), parts along dimension 0
- new_amax: float32 [4, 128], P('ga', 'col'), parts along dimension 0
There are 2 independent parts, one for each index of `ga`. A program takes and returns all parts, laid end to end along the dimension named above; an argument that names none is the same for every part. Nothing has to cross between parts.
All inputs are finite; a program needn't handle non-finite values. No bound on the sum of `pair_mask` on one device may be relied on, other than what follows from the above.
Results may differ from a plain program's by a relative error of at most 0.0065.
Values may be sent and summed in bfloat16 or wider, within the bound.
A program may use at most 128 MiB of HBM per device.

v0:
```python
import functools

import jax
import jax.numpy as jnp
from jax import lax
from jax.experimental import pallas as pl
from jax.experimental.pallas import tpu as pltpu
from jax.sharding import PartitionSpec as P

epsilon = 1e-05
format_limit = 448.0
LANES = 128
f32, bf16 = jnp.float32, jnp.bfloat16
MESH = pl.DeviceIdType.MESH


def kernel(
    dims,
    rep_ref,
    mask_ref,
    hist_ref,
    hist_smem,
    in_gain_ref,
    in_bias_ref,
    proj_ref,
    gate_ref,
    out_gain_smem,
    out_bias_smem,
    out_weight_ref,
    out_ref,
    amax_ref,
    normed,
    maskf,
    inverse,
    peak,
    left_s,
    right_s,
    left_b,
    right_all,
    own_t,
    send_t,
    recv_t,
    full_t,
    spread_t,
    mix_w,
    ow_pad,
    gating,
    peaks,
    peak_send,
    peak_recv,
    z_send,
    z_recv,
    x_send,
    x_recv,
    c_send,
    c_recv,
):
    nz, ny, rows, cols, half, chunks = dims
    ratio = nz // ny
    channels = 2 * half
    per = LANES // rows
    pairs = -(-half // (2 * per))
    groups = 2 * pairs
    span = per * rows
    slot = LANES // (2 * ratio)
    z, y, col = lax.axis_index("gx"), lax.axis_index("gy"), lax.axis_index("col")
    members = nz * ny
    me = z * ny + y

    barrier = pltpu.get_barrier_semaphore()

    def greet(t, carry):
        peer = lax.rem(me + t, members)
        pl.semaphore_signal(
            barrier, inc=1, device_id={"gx": peer // ny, "gy": lax.rem(peer, ny)}, device_id_type=MESH
        )
        return carry

    lax.fori_loop(1, members, greet, 0)
    pl.semaphore_signal(barrier, inc=1, device_id={"col": 1 - col}, device_id_type=MESH)

    normed[pl.ds(rows * cols, LANES), :] = jnp.zeros((LANES, channels), bf16)
    step_rows = 4

    def norm_step(b, carry):
        values = rep_ref[pl.ds(b * step_rows, step_rows)].reshape(step_rows * cols, channels).astype(f32)
        average = jnp.mean(values, axis=-1, keepdims=True)
        centred = values - average
        var = jnp.mean(jnp.square(centred), axis=-1, keepdims=True)
        result = centred * lax.rsqrt(var + epsilon) * in_gain_ref[...] + in_bias_ref[...]
        start = pl.multiple_of(b * step_rows * cols, 16)
        normed[pl.ds(start, step_rows * cols), :] = result.astype(bf16)
        return carry

    lax.fori_loop(0, rows // step_rows, norm_step, 0)
    maskf[...] = jnp.zeros_like(maskf)
    maskf[:, 0:cols] = mask_ref[...].astype(f32)
    scaled = format_limit / hist_ref[...]
    flipped = jnp.concatenate([scaled[0:1], scaled[1:2]], axis=1)
    flipped = jnp.broadcast_to(flipped, (channels, channels))
    inverse[...] = jnp.transpose(flipped)
    peak[...] = jnp.zeros_like(peak)
    tail = left_s.shape[0] - half * rows
    left_s[pl.ds(half * rows, tail), :] = jnp.zeros((tail, LANES), f32)
    right_s[pl.ds(half * rows, tail), :] = jnp.zeros((tail, LANES), f32)

    def project(side, target):
        base = side * half

        def one(i):
            block = normed[pl.ds(pl.multiple_of(i * cols, 16), LANES), :]
            p = lax.dot_general(
                proj_ref[2 * base : 2 * base + channels, :],
                block,
                (((1,), (1,)), ((), ())),
                preferred_element_type=f32,
            )
            value = jax.nn.sigmoid(p[half:]) * p[:half] * maskf[pl.ds(i, 1), :]
            target[pl.ds(i, half, stride=rows), :] = jnp.clip(
                value * inverse[base : base + half, :], -format_limit, format_limit
            )
            return jnp.abs(value)

        def step(b, top):
            for u in range(4):
                top = jnp.maximum(top, one(b * 4 + u))
            return top

        top = lax.fori_loop(0, rows // 4, step, jnp.zeros((half, LANES), f32))
        peak[base : base + half, :] = top

    project(1, right_s)
    bounds = [pairs * c // chunks for c in range(chunks + 1)]

    def z_copy(source, c, direction):
        window = pl.ds(2 * bounds[c], 2 * (bounds[c + 1] - bounds[c]))
        toward = z + 1 if direction == 0 else z - 1
        return pltpu.make_async_remote_copy(
            src_ref=right_all.at[source, window],
            dst_ref=right_all.at[source, window],
            send_sem=z_send.at[direction, source, c],
            recv_sem=z_recv.at[source, c],
            device_id={"gx": toward},
            device_id_type=MESH,
        )

    pl.semaphore_wait(barrier, members)
    for c in range(chunks):
        for g in range(2 * bounds[c], 2 * bounds[c + 1]):
            tile = jnp.transpose(right_s[g * span : g * span + LANES, :])
            right_all[z, g] = tile[:cols].astype(bf16)

        @pl.when(z < nz - 1)
        def _():
            z_copy(z, c, 0).start()

        @pl.when(z > 0)
        def _():
            z_copy(z, c, 1).start()

    project(0, left_s)
    for g in range(groups):
        left_b[g] = left_s[g * span : g * span + LANES, :].astype(bf16)

    peaks[me] = jnp.broadcast_to(jnp.max(jnp.transpose(peak[...]), axis=0, keepdims=True), (8, channels))

    def spread_peak(t, carry):
        peer = lax.rem(me + t, members)
        pltpu.make_async_remote_copy(
            src_ref=peaks.at[me],
            dst_ref=peaks.at[me],
            send_sem=peak_send,
            recv_sem=peak_recv,
            device_id={"gx": peer // ny, "gy": lax.rem(peer, ny)},
            device_id_type=MESH,
        ).start()
        return carry

    lax.fori_loop(1, members, spread_peak, 0)

    lane = lax.broadcasted_iota(jnp.int32, (rows, LANES), 1)

    def triangle_pair(r, p):
        halves = []
        for u in range(2):
            res = lax.dot_general(
                left_b[2 * p + u][:, :cols],
                right_all[r, 2 * p + u],
                (((1,), (0,)), ((), ())),
                preferred_element_type=f32,
            )
            t = res[:rows]
            for s in range(1, per):
                t = jnp.where(lane >= s * rows, res[s * rows : (s + 1) * rows], t)
            halves.append(t)
        return jnp.concatenate(halves, axis=0)

    def x_copy(target, sub, c, source):
        window = pl.ds(bounds[c], bounds[c + 1] - bounds[c])
        return pltpu.make_async_remote_copy(
            src_ref=send_t.at[target, sub, window],
            dst_ref=recv_t.at[source, sub, window],
            send_sem=x_send.at[target, sub, c],
            recv_sem=x_recv.at[source, sub, c],
            device_id={"gy": target},
            device_id_type=MESH,
        )

    def triangle_block(r, c):
        owner, sub = r // ratio, lax.rem(r, ratio)

        @pl.when(owner == y)
        def _():
            for p in range(bounds[c], bounds[c + 1]):
                own_t[sub, p] = triangle_pair(r, p)

        @pl.when(owner != y)
        def _():
            for p in range(bounds[c], bounds[c + 1]):
                send_t[owner, sub, p] = triangle_pair(r, p).astype(bf16)
            x_copy(owner, sub, c, y).start()

    def own_block(c):
        triangle_block(z, c)

    for c in range(chunks):
        own_block(c)

    def gate_step(b, carry):
        for u in range(4):
            i = b * 4 + u
            block = normed[pl.ds(pl.multiple_of(i * cols, 16), LANES), :]
            gating[i] = jax.nn.sigmoid(
                lax.dot_general(
                    gate_ref[...], block, (((1,), (1,)), ((), ())), preferred_element_type=f32
                )
            )
        return carry

    lax.fori_loop(0, rows // 4, gate_step, 0)
    ow_pad[...] = jnp.zeros_like(ow_pad)
    stretch = ow_pad.shape[0] // 2
    square = jnp.concatenate(
        [out_weight_ref[...].astype(f32), jnp.zeros((LANES - half, channels), f32)], axis=0
    )
    turned = jnp.transpose(square)
    for cc in range(2):
        ow_pad[cc * stretch : cc * stretch + half, :] = turned[cc * half : (cc + 1) * half, :]
    for s in range(per):
        parts = [ow_pad[pl.ds(cc * stretch + s, slot, stride=per), :] for cc in range(2)]
        parts.append(jnp.zeros((LANES - 2 * slot, LANES), f32))
        back = jnp.transpose(jnp.concatenate(parts, axis=0))
        mix_w[s * half : (s + 1) * half, :] = back[:half].astype(bf16)
    spread_t[...] = jnp.zeros_like(spread_t)

    def ring_step(d, carry):
        low, high = z - d, z + d
        for c in range(chunks):

            @pl.when(low >= 0)
            def _():
                z_copy(low, c, 0).wait_recv()

                @pl.when(z < nz - 1)
                def _():
                    z_copy(low, c, 0).start()

            @pl.when(high < nz)
            def _():
                z_copy(high, c, 1).wait_recv()

                @pl.when(z > 0)
                def _():
                    z_copy(high, c, 1).start()

            @pl.when(low >= 0)
            def _():
                triangle_block(low, c)

            @pl.when(high < nz)
            def _():
                triangle_block(high, c)

        return carry

    lax.fori_loop(1, nz - 1, ring_step, 0)

    group_lane = lax.broadcasted_iota(jnp.int32, (1, LANES), 1)

    def lane_vector(scalar_of):
        vector = jnp.full((1, LANES), scalar_of(0), f32)
        for s in range(1, per):
            vector = jnp.where(group_lane >= s * rows, scalar_of(s), vector)
        return vector

    def pair_vector(scalar_of, p):
        parts = []
        for u in range(2):
            g = 2 * p + u
            vector = lane_vector(lambda s: scalar_of(g * per + s))
            parts.append(jnp.broadcast_to(vector, (rows, LANES)))
        return jnp.concatenate(parts, axis=0)

    def scale_of(ch):
        ch = jnp.minimum(ch, half - 1)
        return (hist_smem[0, ch] / format_limit) * (hist_smem[1, ch] / format_limit)

    def c_copy(sub, c):
        window = pl.ds(bounds[c], bounds[c + 1] - bounds[c])
        return pltpu.make_async_remote_copy(
            src_ref=full_t.at[col, sub, window],
            dst_ref=full_t.at[col, sub, window],
            send_sem=c_send.at[sub, c],
            recv_sem=c_recv.at[sub, c],
            device_id={"col": 1 - col},
            device_id_type=MESH,
        )

    def send_sub(sub):
        for c in range(chunks):

            def arrive(t, carry):
                x_copy(y, sub, c, lax.rem(y + t, ny)).wait_recv()
                return carry

            lax.fori_loop(1, ny, arrive, 0)

            def finish(p, carry):
                total = own_t[sub, p]
                for t in range(1, ny):
                    total = total + recv_t[lax.rem(y + t, ny), sub, p].astype(f32)
                full_t[col, sub, p] = (total * pair_vector(scale_of, p)).astype(bf16)
                return carry

            lax.fori_loop(bounds[c], bounds[c + 1], finish, 0)
            c_copy(sub, c).start()

    row_at = lax.broadcasted_iota(jnp.int32, (2 * rows, LANES), 0) // rows
    lane_at = lax.broadcasted_iota(jnp.int32, (2 * rows, LANES), 1) // rows
    valid = (((pairs - 1) * 2 + row_at) * per + lane_at) < half

    def segment_mean(pair_sum):
        x = pair_sum[:rows] + pair_sum[rows:]
        total = x
        for s in range(1, per):
            total = total + pltpu.roll(x, s * rows, 1)
        result = total
        for s in range(1, per):
            moved = pltpu.roll(total, LANES - s * rows, 1)
            result = jnp.where(lane < (per - s) * rows, moved, result)
        result = result * (1.0 / channels)
        return jnp.concatenate([result, result], axis=0)

    def norm_sub(sub):
        for c in range(chunks):
            c_copy(sub, c).wait_recv()

        def add_up(p, total):
            return total + full_t[0, sub, p].astype(f32) + full_t[1, sub, p].astype(f32)

        zero = jnp.zeros((2 * rows, LANES), f32)
        mean = segment_mean(lax.fori_loop(0, pairs, add_up, zero))

        def add_squares(p, total):
            for cc in range(2):
                total = total + jnp.square(full_t[cc, sub, p].astype(f32) - mean)
            return total

        squares = lax.fori_loop(0, pairs - 1, add_squares, zero)
        for cc in range(2):
            last = jnp.square(full_t[cc, sub, pairs - 1].astype(f32) - mean)
            squares = squares + jnp.where(valid, last, 0.0)
        factor = lax.rsqrt(segment_mean(squares) + epsilon)

        def normalise(p, carry):
            for cc in range(2):

                def gain_of(ch, cc=cc):
                    return out_gain_smem[cc * half + jnp.minimum(ch, half - 1)]

                def bias_of(ch, cc=cc):
                    return out_bias_smem[cc * half + jnp.minimum(ch, half - 1)]

                t = (full_t[cc, sub, p].astype(f32) - mean) * factor
                t = t * pair_vector(gain_of, p) + pair_vector(bias_of, p)
                for u in range(2):
                    at = (sub * 2 + cc) * slot + 2 * p + u
                    spread_t[pl.ds(at, rows, stride=LANES), :] = t[u * rows : (u + 1) * rows]
            return carry

        lax.fori_loop(0, pairs, normalise, 0)

    order = jnp.where(2 * z >= nz, ratio - 1, 0)
    step_sign = jnp.where(2 * z >= nz, -1, 1)
    for t in range(ratio - 1):
        send_sub(order + step_sign * t)
    for t in range(ratio - 1):
        norm_sub(order + step_sign * t)
    ring_step(nz - 1, 0)
    send_sub(order + step_sign * (ratio - 1))
    norm_sub(order + step_sign * (ratio - 1))

    wide = lax.broadcasted_iota(jnp.int32, (half, LANES), 1)

    def mix_one(i):
        start = pl.multiple_of(i * LANES, LANES)
        tile = spread_t[pl.ds(start, LANES), :].astype(bf16)
        parts = [tile[rr * 2 * slot : (rr + 1) * 2 * slot] for rr in range(ratio)]
        res = jnp.dot(
            mix_w[:, 0 : 2 * slot], jnp.concatenate(parts, axis=1), preferred_element_type=f32
        )
        mixing = None
        for rr in range(ratio):
            total = None
            for s in range(per):
                piece = res[s * half : (s + 1) * half, rr * LANES : (rr + 1) * LANES]
                shift = (rr - s) * rows % LANES
                piece = pltpu.roll(piece, shift, 1) if shift else piece
                total = piece if total is None else total + piece
            mixing = total if mixing is None else jnp.where(wide >= rr * rows, total, mixing)
        out_ref[i] = (gating[i] * mixing)[:, :cols].astype(bf16)

    def mix_step(b, carry):
        for u in range(4):
            mix_one(b * 4 + u)
        return carry

    lax.fori_loop(0, rows // 4, mix_step, 0)

    others = peaks.at[pl.ds(0, members - 1)]
    pltpu.make_async_copy(others, others, peak_recv).wait()
    top = jnp.max(jnp.max(peaks[...], axis=0), axis=0, keepdims=True)
    amax_ref[0:1, :] = top[:, :half]
    amax_ref[1:2, :] = top[:, half:]

    pltpu.make_async_copy(others, others, peak_send).wait()
    for sub in range(ratio):
        for c in range(chunks):
            c_copy(sub, c).wait_send()

    def drain_x(t, carry):
        for sub in range(ratio):
            for c in range(chunks):
                x_copy(lax.rem(y + t, ny), sub, c, y).wait_send()
        return carry

    lax.fori_loop(1, ny, drain_x, 0)

    def drain_z(source, carry):
        for c in range(chunks):

            @pl.when((source <= z) & (z < nz - 1))
            def _():
                z_copy(source, c, 0).wait_send()

            @pl.when((source >= z) & (z > 0))
            def _():
                z_copy(source, c, 1).wait_send()

        return carry

    lax.fori_loop(0, nz, drain_z, 0)


def on_device(
    nz,
    ny,
    pair_rep,
    pair_mask,
    amax_history,
    in_gain,
    in_bias,
    proj_weight,
    gate_weight,
    out_gain,
    out_bias,
    out_weight,
):
    crops, rows, cols, channels = pair_rep.shape
    half = proj_weight.shape[2]
    chunks = 2
    ratio = nz // ny
    per = LANES // rows
    pairs = -(-half // (2 * per))
    groups = 2 * pairs
    slot = LANES // (2 * ratio)
    members = nz * ny
    weights = jnp.transpose(proj_weight, (1, 2, 0)).reshape(4 * half, channels)
    scratch_rows = -(-((groups - 1) * per * rows + LANES) // 8) * 8
    dma = pltpu.SemaphoreType.DMA
    vmem = pl.BlockSpec(memory_space=pltpu.VMEM)
    smem = pl.BlockSpec(memory_space=pltpu.SMEM)
    tile = (2 * rows, LANES)
    update, new_amax = pl.pallas_call(
        functools.partial(kernel, (nz, ny, rows, cols, half, chunks)),
        out_shape=(
            jax.ShapeDtypeStruct((rows, half, cols), bf16),
            jax.ShapeDtypeStruct((2, half), f32),
        ),
        in_specs=[vmem, vmem, vmem, smem, vmem, vmem, vmem, vmem, smem, smem, vmem],
        out_specs=(vmem, vmem),
        scratch_shapes=[
            pltpu.VMEM((rows * cols + LANES, channels), bf16),
            pltpu.VMEM((rows, LANES), f32),
            pltpu.VMEM((channels, LANES), f32),
            pltpu.VMEM((channels, LANES), f32),
            pltpu.VMEM((scratch_rows, LANES), f32),
            pltpu.VMEM((scratch_rows, LANES), f32),
            pltpu.VMEM((groups, LANES, LANES), bf16),
            pltpu.VMEM((nz, groups, cols, LANES), bf16),
            pltpu.VMEM((ratio, pairs) + tile, f32),
            pltpu.VMEM((ny, ratio, pairs) + tile, bf16),
            pltpu.VMEM((ny, ratio, pairs) + tile, bf16),
            pltpu.VMEM((2, ratio, pairs) + tile, bf16),
            pltpu.VMEM((rows * LANES, LANES), f32),
            pltpu.VMEM((per * half, LANES), bf16),
            pltpu.VMEM((2 * slot * per, LANES), f32),
            pltpu.VMEM((rows, half, LANES), f32),
            pltpu.VMEM((members, 8, channels), f32),
            dma,
            dma,
            dma((2, nz, chunks)),
            dma((nz, chunks)),
            dma((ny, ratio, chunks)),
            dma((ny, ratio, chunks)),
            dma((ratio, chunks)),
            dma((ratio, chunks)),
        ],
        compiler_params=pltpu.CompilerParams(
            collective_id=0, has_side_effects=True, vmem_limit_bytes=56 * 1024 * 1024
        ),
    )(
        pair_rep[0],
        pair_mask[0],
        amax_history,
        amax_history,
        in_gain.reshape(1, channels),
        in_bias.reshape(1, channels),
        weights,
        gate_weight.T,
        out_gain,
        out_bias,
        out_weight.T,
    )
    return jnp.transpose(update, (0, 2, 1))[None], new_amax


def solution(mesh):
    placed = (
        P("ga", "gx", "gy", None),
        P("ga", "gx", "gy"),
        P(None, "col"),
        P(),
        P(),
        P(None, None, "col"),
        P(None, "col"),
        P(),
        P(),
        P(None, "col"),
    )
    return jax.shard_map(
        functools.partial(on_device, mesh.shape["gx"], mesh.shape["gy"]),
        mesh=mesh,
        in_specs=placed,
        out_specs=(P("ga", "gx", "gy", "col"), P("ga", "col")),
        check_vma=False,
    )
```

profile of v0, /device:TPU:3, one launch (start us, length us, event | category | flops | bytes accessed | tf_op | source)
XLA Modules:
  0.0 52.9 jit_solution(2736983451841253226)
XLA Ops:
  0.6 49.7 %shard_map.113 = (bf16[40,64,80]{2,1,0:T(8,128)(2,1)}, f32[2,64]{1,0:T(2,128)}) custom-call(bf16[40,80,128]{2,1,0:T(8,128)(2,1)} %bitcast.12, s32[40,80]{1,0:T(8,128)} %bitcast.15, f32[2,64]{1,0:T(2,128)} %hist_smem.1, f32[2,64]{1,0:T(2,128)} %hist_smem.1, f32[1,128]{1,0:T(1,128)} %bitcast.18, f32[1,128]{1,0:T(1,128)} %bitcast.19, ...), custom_call_target="tpu_custom_call" | custom-call | tf_op jit(solution)/shard_map/pallas_call | solution.py:494
  50.4 0.0 copy-start
  50.4 2.0 %copy.14 = bf16[1,40,80,64]{2,3,1,0:T(8,128)(2,1)} copy(bf16[1,40,80,64]{2,3,1,0:T(8,128)(2,1)} %bitcast.13) | data formatting | bytes 819200
  52.4 0.0 copy-done
  52.4 0.6 %copy.15 = f32[2,64]{1,0:T(2,128)} copy(f32[2,64]{1,0:T(2,128)S(1)} %copy-done) | data formatting | bytes 1024
Async XLA Ops:
  50.4 2.0 %copy-start = (f32[2,64]{1,0:T(2,128)S(1)}, f32[2,64]{1,0:T(2,128)}, u32[]{:S(2)}) copy-start(f32[2,64]{1,0:T(2,128)} %get-tuple-element.9) | copy-start | bytes 1540
where the time goes:
time: 53.1 us; the launch traced here: 52.9 us
  Pallas kernels  49.7 us (94%)
  local copies, waits for them, and re-layouts  2.53 us (5%)
  between operations  0.65 us (1%)
    pallas_call x1, Pallas kernels, on_device(): pl.pallas_call(functools.partial(kernel, (nz, ny, rows, cols, half, chunk...  49.7 us
    unnamed x4, local copies, waits for them, and re-layouts  2.53 us

commit v1 on v0

--- a/solution.py
+++ b/solution.py
@@ -36,24 +36,33 @@
     left_s,
     right_s,
     left_b,
+    left_t,
+    left_r,
+    left_e,
     right_all,
     own_t,
     send_t,
     recv_t,
+    ret_t,
     full_t,
     spread_t,
     mix_w,
     ow_pad,
+    vecs,
     gating,
     peaks,
     peak_send,
     peak_recv,
     z_send,
     z_recv,
+    l_send,
+    l_recv,
     x_send,
     x_recv,
     c_send,
     c_recv,
+    e_send,
+    e_recv,
 ):
     nz, ny, rows, cols, half, chunks = dims
     ratio = nz // ny
@@ -66,6 +75,15 @@
     z, y, col = lax.axis_index("gx"), lax.axis_index("gy"), lax.axis_index("col")
     members = nz * ny
     me = z * ny + y
+    is_end = (z == 0) | (z == nz - 1)
+    is_next = (z == 1) | (z == nz - 2)
+    high_side = 2 * z >= nz
+    sgn = jnp.where(high_side, 1, -1)
+    end = jnp.where(high_side, nz - 1, 0)
+    inward = jnp.where(high_side, 1, 0)
+    up_ok = z <= nz - 3
+    down_ok = z >= 2
+    unroll = max(u for u in range(1, 9) if rows % u == 0)
 
     barrier = pltpu.get_barrier_semaphore()
 
@@ -79,8 +97,14 @@
     lax.fori_loop(1, members, greet, 0)
     pl.semaphore_signal(barrier, inc=1, device_id={"col": 1 - col}, device_id_type=MESH)
 
+    @pl.when(is_end)
+    def _():
+        pl.semaphore_signal(
+            barrier, inc=1, device_id={"gx": z - sgn, "col": 1 - col}, device_id_type=MESH
+        )
+
     normed[pl.ds(rows * cols, LANES), :] = jnp.zeros((LANES, channels), bf16)
-    step_rows = 4
+    step_rows = unroll
 
     def norm_step(b, carry):
         values = rep_ref[pl.ds(b * step_rows, step_rows)].reshape(step_rows * cols, channels).astype(f32)
@@ -122,11 +146,11 @@
             return jnp.abs(value)
 
         def step(b, top):
-            for u in range(4):
-                top = jnp.maximum(top, one(b * 4 + u))
+            for u in range(unroll):
+                top = jnp.maximum(top, one(b * unroll + u))
             return top
 
-        top = lax.fori_loop(0, rows // 4, step, jnp.zeros((half, LANES), f32))
+        top = lax.fori_loop(0, rows // unroll, step, jnp.zeros((half, LANES), f32))
         peak[base : base + half, :] = top
 
     project(1, right_s)
@@ -134,7 +158,7 @@
 
     def z_copy(source, c, direction):
         window = pl.ds(2 * bounds[c], 2 * (bounds[c + 1] - bounds[c]))
-        toward = z + 1 if direction == 0 else z - 1
+        toward = z + 1 - 2 * direction
         return pltpu.make_async_remote_copy(
             src_ref=right_all.at[source, window],
             dst_ref=right_all.at[source, window],
@@ -144,21 +168,45 @@
             device_id_type=MESH,
         )
 
-    pl.semaphore_wait(barrier, members)
+    def left_copy(c):
+        window = pl.ds(2 * bounds[c], 2 * (bounds[c + 1] - bounds[c]))
+        return pltpu.make_async_remote_copy(
+            src_ref=left_t.at[window],
+            dst_ref=left_r.at[window],
+            send_sem=l_send.at[c],
+            recv_sem=l_recv.at[c],
+            device_id={"gx": z - sgn},
+            device_id_type=MESH,
+        )
+
+    pl.semaphore_wait(barrier, members + jnp.where(is_next, 1, 0))
+    early = chunks // 2
     for c in range(chunks):
         for g in range(2 * bounds[c], 2 * bounds[c + 1]):
             tile = jnp.transpose(right_s[g * span : g * span + LANES, :])
             right_all[z, g] = tile[:cols].astype(bf16)
-
-        @pl.when(z < nz - 1)
+        now = True if c < early else jnp.logical_not(is_end)
+
+        @pl.when(up_ok & now)
         def _():
             z_copy(z, c, 0).start()
 
-        @pl.when(z > 0)
+        @pl.when(down_ok & now)
         def _():
             z_copy(z, c, 1).start()
 
     project(0, left_s)
+
+    @pl.when(is_end)
+    def _():
+        for c in range(chunks):
+            for g in range(2 * bounds[c], 2 * bounds[c + 1]):
+                tile = jnp.transpose(left_s[g * span : g * span + LANES, :])
+                left_t[g] = tile[:cols].astype(bf16)
+            if c >= early:
+                z_copy(z, c, inward).start()
+            left_copy(c).start()
+
     for g in range(groups):
         left_b[g] = left_s[g * span : g * span + LANES, :].astype(bf16)
 
@@ -180,11 +228,11 @@
 
     lane = lax.broadcasted_iota(jnp.int32, (rows, LANES), 1)
 
-    def triangle_pair(r, p):
+    def triangle_pair(lhs, r, p):
         halves = []
         for u in range(2):
             res = lax.dot_general(
-                left_b[2 * p + u][:, :cols],
+                lhs[2 * p + u][:, :cols],
                 right_all[r, 2 * p + u],
                 (((1,), (0,)), ((), ())),
                 preferred_element_type=f32,
@@ -195,40 +243,36 @@
             halves.append(t)
         return jnp.concatenate(halves, axis=0)
 
-    def x_copy(target, sub, c, source):
+    def x_copy(rowset, target, sub, c, source):
         window = pl.ds(bounds[c], bounds[c + 1] - bounds[c])
         return pltpu.make_async_remote_copy(
-            src_ref=send_t.at[target, sub, window],
-            dst_ref=recv_t.at[source, sub, window],
-            send_sem=x_send.at[target, sub, c],
-            recv_sem=x_recv.at[source, sub, c],
+            src_ref=send_t.at[rowset, target, sub, window],
+            dst_ref=recv_t.at[rowset, source, sub, window],
+            send_sem=x_send.at[rowset, target, sub, c],
+            recv_sem=x_recv.at[rowset, source, sub, c],
             device_id={"gy": target},
             device_id_type=MESH,
         )
 
-    def triangle_block(r, c):
+    def triangle_block(rowset, r, c):
         owner, sub = r // ratio, lax.rem(r, ratio)
-
-        @pl.when(owner == y)
-        def _():
-            for p in range(bounds[c], bounds[c + 1]):
-                own_t[sub, p] = triangle_pair(r, p)
+        slot = jnp.where(owner == y, sub, ratio)
+        lhs = left_e if rowset else left_b
+        for p in range(bounds[c], bounds[c + 1]):
+            t = triangle_pair(lhs, r, p)
+            own_t[rowset, slot, p] = t
+            send_t[rowset, owner, sub, p] = t.astype(bf16)
 
         @pl.when(owner != y)
         def _():
-            for p in range(bounds[c], bounds[c + 1]):
-                send_t[owner, sub, p] = triangle_pair(r, p).astype(bf16)
-            x_copy(owner, sub, c, y).start()
-
-    def own_block(c):
-        triangle_block(z, c)
+            x_copy(rowset, owner, sub, c, y).start()
 
     for c in range(chunks):
-        own_block(c)
+        triangle_block(0, z, c)
 
     def gate_step(b, carry):
-        for u in range(4):
-            i = b * 4 + u
+        for u in range(unroll):
+            i = b * unroll + u
             block = normed[pl.ds(pl.multiple_of(i * cols, 16), LANES), :]
             gating[i] = jax.nn.sigmoid(
                 lax.dot_general(
@@ -237,7 +281,7 @@
             )
         return carry
 
-    lax.fori_loop(0, rows // 4, gate_step, 0)
+    lax.fori_loop(0, rows // unroll, gate_step, 0)
     ow_pad[...] = jnp.zeros_like(ow_pad)
     stretch = ow_pad.shape[0] // 2
     square = jnp.concatenate(
@@ -253,57 +297,30 @@
         mix_w[s * half : (s + 1) * half, :] = back[:half].astype(bf16)
     spread_t[...] = jnp.zeros_like(spread_t)
 
-    def ring_step(d, carry):
-        low, high = z - d, z + d
-        for c in range(chunks):
-
-            @pl.when(low >= 0)
-            def _():
-                z_copy(low, c, 0).wait_recv()
-
-                @pl.when(z < nz - 1)
-                def _():
-                    z_copy(low, c, 0).start()
-
-            @pl.when(high < nz)
-            def _():
-                z_copy(high, c, 1).wait_recv()
-
-                @pl.when(z > 0)
-                def _():
-                    z_copy(high, c, 1).start()
-
-            @pl.when(low >= 0)
-            def _():
-                triangle_block(low, c)
-
-            @pl.when(high < nz)
-            def _():
-                triangle_block(high, c)
-
+    group_lane = lax.broadcasted_iota(jnp.int32, (1, LANES), 1)
+
+    def lane_vector(scalar_of, g):
+        ch = [jnp.minimum(g * per + s, half - 1) for s in range(per)]
+        vector = jnp.full((1, LANES), scalar_of(ch[0]), f32)
+        for s in range(1, per):
+            vector = jnp.where(group_lane >= s * rows, scalar_of(ch[s]), vector)
+        return vector
+
+    def scale_of(ch):
+        return (hist_smem[0, ch] / format_limit) * (hist_smem[1, ch] / format_limit)
+
+    def fill_vectors(g, carry):
+        vecs[0, pl.ds(g, 1), :] = lane_vector(scale_of, g)
+        for cc in range(2):
+            vecs[1 + cc, pl.ds(g, 1), :] = lane_vector(lambda ch: out_gain_smem[cc * half + ch], g)
+            vecs[3 + cc, pl.ds(g, 1), :] = lane_vector(lambda ch: out_bias_smem[cc * half + ch], g)
         return carry
 
-    lax.fori_loop(1, nz - 1, ring_step, 0)
-
-    group_lane = lax.broadcasted_iota(jnp.int32, (1, LANES), 1)
-
-    def lane_vector(scalar_of):
-        vector = jnp.full((1, LANES), scalar_of(0), f32)
-        for s in range(1, per):
-            vector = jnp.where(group_lane >= s * rows, scalar_of(s), vector)
-        return vector
-
-    def pair_vector(scalar_of, p):
-        parts = []
-        for u in range(2):
-            g = 2 * p + u
-            vector = lane_vector(lambda s: scalar_of(g * per + s))
-            parts.append(jnp.broadcast_to(vector, (rows, LANES)))
+    lax.fori_loop(0, groups, fill_vectors, 0)
+
+    def pair_vector(v, p):
+        parts = [jnp.broadcast_to(vecs[v, 2 * p + u : 2 * p + u + 1, :], (rows, LANES)) for u in range(2)]
         return jnp.concatenate(parts, axis=0)
-
-    def scale_of(ch):
-        ch = jnp.minimum(ch, half - 1)
-        return (hist_smem[0, ch] / format_limit) * (hist_smem[1, ch] / format_limit)
 
     def c_copy(sub, c):
         window = pl.ds(bounds[c], bounds[c + 1] - bounds[c])
@@ -316,24 +333,44 @@
             device_id_type=MESH,
         )
 
-    def send_sub(sub):
-        for c in range(chunks):
-
+    def end_copy(sub, c, source, target):
+        window = pl.ds(bounds[c], bounds[c + 1] - bounds[c])
+        return pltpu.make_async_remote_copy(
+            src_ref=ret_t.at[sub, window],
+            dst_ref=full_t.at[source, sub, window],
+            send_sem=e_send.at[target, sub, c],
+            recv_sem=e_recv.at[source, sub, c],
+            device_id={"gx": end, "col": target},
+            device_id_type=MESH,
+        )
+
+    def finish_block(rowset, r, c):
+        owner, sub = r // ratio, lax.rem(r, ratio)
+
+        @pl.when(owner == y)
+        def _():
             def arrive(t, carry):
-                x_copy(y, sub, c, lax.rem(y + t, ny)).wait_recv()
+                x_copy(rowset, y, sub, c, lax.rem(y + t, ny)).wait_recv()
                 return carry
 
             lax.fori_loop(1, ny, arrive, 0)
-
-            def finish(p, carry):
-                total = own_t[sub, p]
+            for p in range(bounds[c], bounds[c + 1]):
+                total = own_t[rowset, sub, p]
                 for t in range(1, ny):
-                    total = total + recv_t[lax.rem(y + t, ny), sub, p].astype(f32)
-                full_t[col, sub, p] = (total * pair_vector(scale_of, p)).astype(bf16)
-                return carry
-
-            lax.fori_loop(bounds[c], bounds[c + 1], finish, 0)
-            c_copy(sub, c).start()
+                    total = total + recv_t[rowset, lax.rem(y + t, ny), sub, p].astype(f32)
+                result = (total * pair_vector(0, p)).astype(bf16)
+                if rowset:
+                    ret_t[sub, p] = result
+                else:
+                    full_t[col, sub, p] = result
+            if rowset:
+                end_copy(sub, c, col, col).start()
+                end_copy(sub, c, col, 1 - col).start()
+            else:
+                c_copy(sub, c).start()
+
+    for c in range(chunks):
+        finish_block(0, z, c)
 
     row_at = lax.broadcasted_iota(jnp.int32, (2 * rows, LANES), 0) // rows
     lane_at = lax.broadcasted_iota(jnp.int32, (2 * rows, LANES), 1) // rows
@@ -352,53 +389,129 @@
         return jnp.concatenate([result, result], axis=0)
 
     def norm_sub(sub):
-        for c in range(chunks):
-            c_copy(sub, c).wait_recv()
-
-        def add_up(p, total):
-            return total + full_t[0, sub, p].astype(f32) + full_t[1, sub, p].astype(f32)
-
-        zero = jnp.zeros((2 * rows, LANES), f32)
-        mean = segment_mean(lax.fori_loop(0, pairs, add_up, zero))
-
-        def add_squares(p, total):
+        r = y * ratio + sub
+        returned = is_end & (r != z)
+
+        @pl.when(returned)
+        def _():
+            for c in range(chunks):
+                for cc in range(2):
+                    end_copy(sub, c, cc, col).wait_recv()
+
+        @pl.when(jnp.logical_not(returned))
+        def _():
+            for c in range(chunks):
+                c_copy(sub, c).wait_recv()
+
+        total = jnp.zeros((2 * rows, LANES), f32)
+        for p in range(pairs):
+            total = total + full_t[0, sub, p].astype(f32) + full_t[1, sub, p].astype(f32)
+        mean = segment_mean(total)
+        squares = jnp.zeros((2 * rows, LANES), f32)
+        for p in range(pairs):
             for cc in range(2):
-                total = total + jnp.square(full_t[cc, sub, p].astype(f32) - mean)
-            return total
-
-        squares = lax.fori_loop(0, pairs - 1, add_squares, zero)
-        for cc in range(2):
-            last = jnp.square(full_t[cc, sub, pairs - 1].astype(f32) - mean)
-            squares = squares + jnp.where(valid, last, 0.0)
+                square = jnp.square(full_t[cc, sub, p].astype(f32) - mean)
+                if p == pairs - 1:
+                    square = jnp.where(valid, square, 0.0)
+                squares = squares + square
         factor = lax.rsqrt(segment_mean(squares) + epsilon)
-
-        def normalise(p, carry):
+        for p in range(pairs):
             for cc in range(2):
-
-                def gain_of(ch, cc=cc):
-                    return out_gain_smem[cc * half + jnp.minimum(ch, half - 1)]
-
-                def bias_of(ch, cc=cc):
-                    return out_bias_smem[cc * half + jnp.minimum(ch, half - 1)]
-
                 t = (full_t[cc, sub, p].astype(f32) - mean) * factor
-                t = t * pair_vector(gain_of, p) + pair_vector(bias_of, p)
+                t = t * pair_vector(1 + cc, p) + pair_vector(3 + cc, p)
                 for u in range(2):
                     at = (sub * 2 + cc) * slot + 2 * p + u
                     spread_t[pl.ds(at, rows, stride=LANES), :] = t[u * rows : (u + 1) * rows]
+
+    first_low = jnp.logical_xor(2 * y < ny, is_end)
+    order = jnp.where(first_low, ratio - 1, 0)
+    step_sign = jnp.where(first_low, -1, 1)
+
+    end_sequence = [("right", c) for c in range(early)] + [("left", c) for c in range(early)]
+    for c in range(early, chunks):
+        end_sequence += [("right", c), ("left", c)]
+    within = nz == 4 and ratio == 2
+
+    @pl.when(is_next)
+    def _():
+        lefts, held, pending = [], [], []
+        for s in range(2 * chunks):
+            kind, ce = end_sequence[s]
+            k, c = 1 + s // chunks, s % chunks
+            source = z - sgn * k
+            todo = []
+            if kind == "right":
+                z_copy(end, ce, inward).wait_recv()
+                z_copy(end, ce, inward).start()
+            if within and s == 2 * chunks - 1:
+                norm_sub(order)
+            z_copy(source, c, 1 - inward).wait_recv()
+            if kind == "left":
+                left_copy(ce).wait_recv()
+                for g in range(2 * bounds[ce], 2 * bounds[ce + 1]):
+                    tile = jnp.concatenate(
+                        [left_r[g].astype(f32), jnp.zeros((LANES - cols, LANES), f32)], axis=0
+                    )
+                    left_e[g] = jnp.transpose(tile).astype(bf16)
+                lefts.append(ce)
+            if c in lefts:
+                todo.append((1, source, c))
+            todo.append((0, source, c))
+            if kind == "left":
+                todo += [(1, z - sgn * kk, ce) for kk, cc in held if cc == ce]
+                todo.append((1, z, ce))
+            else:
+                todo.append((0, end, ce))
+            held.append((k, c))
+            for block in todo:
+                triangle_block(*block)
+            for block in pending:
+                finish_block(*block)
+            pending = todo
+        for block in pending:
+            finish_block(*block)
+
+        def farther(k, carry):
+            for c in range(chunks):
+                z_copy(z - sgn * k, c, 1 - inward).wait_recv()
+                for rowset in (1, 0):
+                    triangle_block(rowset, z - sgn * k, c)
+                for rowset in (1, 0):
+                    finish_block(rowset, z - sgn * k, c)
             return carry
 
-        lax.fori_loop(0, pairs, normalise, 0)
-
-    order = jnp.where(2 * z >= nz, ratio - 1, 0)
-    step_sign = jnp.where(2 * z >= nz, -1, 1)
-    for t in range(ratio - 1):
-        send_sub(order + step_sign * t)
-    for t in range(ratio - 1):
-        norm_sub(order + step_sign * t)
-    ring_step(nz - 1, 0)
-    send_sub(order + step_sign * (ratio - 1))
-    norm_sub(order + step_sign * (ratio - 1))
+        if nz > 4:
+            lax.fori_loop(3, nz - 1, farther, 0)
+
+    if nz > 4:
+
+        @pl.when(jnp.logical_not(is_end | is_next))
+        def _():
+            def ring_step(d, carry):
+                for c in range(chunks):
+                    for source, direction, there in ((z - d, 0, z - d >= 0), (z + d, 1, z + d < nz)):
+
+                        @pl.when(there)
+                        def _(source=source, direction=direction, c=c):
+                            z_copy(source, c, direction).wait_recv()
+                            z_copy(source, c, direction).start()
+                            triangle_block(0, source, c)
+                            finish_block(0, source, c)
+
+                return carry
+
+            lax.fori_loop(1, nz - 1, ring_step, 0)
+
+    if within:
+
+        @pl.when(is_end)
+        def _():
+            norm_sub(order)
+
+        norm_sub(order + step_sign)
+    else:
+        for t in range(ratio):
+            norm_sub(order + step_sign * t)
 
     wide = lax.broadcasted_iota(jnp.int32, (half, LANES), 1)
 
@@ -421,11 +534,11 @@
         out_ref[i] = (gating[i] * mixing)[:, :cols].astype(bf16)
 
     def mix_step(b, carry):
-        for u in range(4):
-            mix_one(b * 4 + u)
+        for u in range(unroll):
+            mix_one(b * unroll + u)
         return carry
 
-    lax.fori_loop(0, rows // 4, mix_step, 0)
+    lax.fori_loop(0, rows // unroll, mix_step, 0)
 
     others = peaks.at[pl.ds(0, members - 1)]
     pltpu.make_async_copy(others, others, peak_recv).wait()
@@ -434,27 +547,54 @@
     amax_ref[1:2, :] = top[:, half:]
 
     pltpu.make_async_copy(others, others, peak_send).wait()
+
     for sub in range(ratio):
+        r = y * ratio + sub
+
+        @pl.when(jnp.logical_not(is_end) | (r == z))
+        def _(sub=sub):
+            for c in range(chunks):
+                c_copy(sub, c).wait_send()
+
+        @pl.when(is_next & (r != end))
+        def _(sub=sub):
+            for c in range(chunks):
+                for target in range(2):
+                    end_copy(sub, c, col, target).wait_send()
+
+    def drain_x(t, carry):
+        target = lax.rem(y + t, ny)
+        for sub in range(ratio):
+            r = target * ratio + sub
+
+            @pl.when(jnp.logical_not(is_end) | (r == z))
+            def _(sub=sub):
+                for c in range(chunks):
+                    x_copy(0, target, sub, c, y).wait_send()
+
+            @pl.when(is_next & (r != end))
+            def _(sub=sub):
+                for c in range(chunks):
+                    x_copy(1, target, sub, c, y).wait_send()
+
+        return carry
+
+    lax.fori_loop(1, ny, drain_x, 0)
+
+    @pl.when(is_end)
+    def _():
         for c in range(chunks):
-            c_copy(sub, c).wait_send()
-
-    def drain_x(t, carry):
-        for sub in range(ratio):
+            left_copy(c).wait_send()
+
+    def drain_z(source, carry):
+        @pl.when((source <= z) & up_ok)
+        def _():
             for c in range(chunks):
-                x_copy(lax.rem(y + t, ny), sub, c, y).wait_send()
-        return carry
-
-    lax.fori_loop(1, ny, drain_x, 0)
-
-    def drain_z(source, carry):
-        for c in range(chunks):
-
-            @pl.when((source <= z) & (z < nz - 1))
-            def _():
                 z_copy(source, c, 0).wait_send()
 
-            @pl.when((source >= z) & (z > 0))
-            def _():
+        @pl.when((source >= z) & down_ok)
+        def _():
+            for c in range(chunks):
                 z_copy(source, c, 1).wait_send()
 
         return carry
@@ -478,7 +618,7 @@
 ):
     crops, rows, cols, channels = pair_rep.shape
     half = proj_weight.shape[2]
-    chunks = 2
+    chunks = 4
     ratio = nz // ny
     per = LANES // rows
     pairs = -(-half // (2 * per))
@@ -507,24 +647,33 @@
             pltpu.VMEM((scratch_rows, LANES), f32),
             pltpu.VMEM((scratch_rows, LANES), f32),
             pltpu.VMEM((groups, LANES, LANES), bf16),
+            pltpu.VMEM((groups, cols, LANES), bf16),
+            pltpu.VMEM((groups, cols, LANES), bf16),
+            pltpu.VMEM((groups, LANES, LANES), bf16),
             pltpu.VMEM((nz, groups, cols, LANES), bf16),
-            pltpu.VMEM((ratio, pairs) + tile, f32),
-            pltpu.VMEM((ny, ratio, pairs) + tile, bf16),
-            pltpu.VMEM((ny, ratio, pairs) + tile, bf16),
+            pltpu.VMEM((2, ratio + 1, pairs) + tile, f32),
+            pltpu.VMEM((2, ny, ratio, pairs) + tile, bf16),
+            pltpu.VMEM((2, ny, ratio, pairs) + tile, bf16),
+            pltpu.VMEM((ratio, pairs) + tile, bf16),
             pltpu.VMEM((2, ratio, pairs) + tile, bf16),
             pltpu.VMEM((rows * LANES, LANES), f32),
             pltpu.VMEM((per * half, LANES), bf16),
             pltpu.VMEM((2 * slot * per, LANES), f32),
+            pltpu.VMEM((5, groups, LANES), f32),
             pltpu.VMEM((rows, half, LANES), f32),
             pltpu.VMEM((members, 8, channels), f32),
             dma,
             dma,
             dma((2, nz, chunks)),
             dma((nz, chunks)),
-            dma((ny, ratio, chunks)),
-            dma((ny, ratio, chunks)),
+            dma((chunks,)),
+            dma((chunks,)),
+            dma((2, ny, ratio, chunks)),
+            dma((2, ny, ratio, chunks)),
             dma((ratio, chunks)),
             dma((ratio, chunks)),
+            dma((2, ratio, chunks)),
+            dma((2, ratio, chunks)),
         ],
         compiler_params=pltpu.CompilerParams(
             collective_id=0, has_side_effects=True, vmem_limit_bytes=56 * 1024 * 1024

time: 53.1 us -> 51.1 us (0.962)
  Pallas kernels: 49.7 us -> 47.8 us
    pallas_call x1, Pallas kernels: 49.7 us -> 47.8 us  [on_device(): pl.pallas_call(functools.partial(kernel, (nz, ny, rows, cols, half, chunk...]
where the time goes in v1:
time: 51.1 us; the launch traced here: 50.9 us
  Pallas kernels  47.8 us (94%)
  local copies, waits for them, and re-layouts  2.53 us (5%)
  between operations  0.65 us (1%)
    pallas_call x1, Pallas kernels, on_device(): pl.pallas_call(functools.partial(kernel, (nz, ny, rows, cols, half, chunk...  47.8 us
    unnamed x4, local copies, waits for them, and re-layouts  2.53 us

profile of v1, /device:TPU:3, one launch (start us, length us, event | category | flops | bytes accessed | tf_op | source)
XLA Modules:
  0.0 50.9 jit_solution(7187677016355566933)
XLA Ops:
  0.6 47.8 %shard_map.113 = (bf16[40,64,80]{2,1,0:T(8,128)(2,1)}, f32[2,64]{1,0:T(2,128)}) custom-call(bf16[40,80,128]{2,1,0:T(8,128)(2,1)} %bitcast.12, s32[40,80]{1,0:T(8,128)} %bitcast.15, f32[2,64]{1,0:T(2,128)} %hist_smem.1, f32[2,64]{1,0:T(2,128)} %hist_smem.1, f32[1,128]{1,0:T(1,128)} %bitcast.18, f32[1,128]{1,0:T(1,128)} %bitcast.19, ...), custom_call_target="tpu_custom_call" | custom-call | tf_op jit(solution)/shard_map/pallas_call | solution.py:634
  48.4 0.0 copy-start
  48.4 2.0 %copy.14 = bf16[1,40,80,64]{2,3,1,0:T(8,128)(2,1)} copy(bf16[1,40,80,64]{2,3,1,0:T(8,128)(2,1)} %bitcast.13) | data formatting | bytes 819200
  50.4 0.0 copy-done
  50.4 0.6 %copy.15 = f32[2,64]{1,0:T(2,128)} copy(f32[2,64]{1,0:T(2,128)S(1)} %copy-done) | data formatting | bytes 1024
Async XLA Ops:
  48.4 2.0 %copy-start = (f32[2,64]{1,0:T(2,128)S(1)}, f32[2,64]{1,0:T(2,128)}, u32[]{:S(2)}) copy-start(f32[2,64]{1,0:T(2,128)} %get-tuple-element.9) | copy-start | bytes 1540

commit v2 on v1

--- a/solution.py
+++ b/solution.py
@@ -27,8 +27,8 @@
     out_gain_smem,
     out_bias_smem,
     out_weight_ref,
-    out_ref,
-    amax_ref,
+    out_hbm,
+    amax_hbm,
     normed,
     maskf,
     inverse,
@@ -46,8 +46,8 @@
     ret_t,
     full_t,
     spread_t,
-    mix_w,
-    ow_pad,
+    out_ref,
+    amax_ref,
     vecs,
     gating,
     peaks,
@@ -63,6 +63,8 @@
     c_recv,
     e_send,
     e_recv,
+    out_sem,
+    amax_sem,
 ):
     nz, ny, rows, cols, half, chunks = dims
     ratio = nz // ny
@@ -71,7 +73,7 @@
     pairs = -(-half // (2 * per))
     groups = 2 * pairs
     span = per * rows
-    slot = LANES // (2 * ratio)
+    pitch = channels + 1
     z, y, col = lax.axis_index("gx"), lax.axis_index("gy"), lax.axis_index("col")
     members = nz * ny
     me = z * ny + y
@@ -81,8 +83,7 @@
     sgn = jnp.where(high_side, 1, -1)
     end = jnp.where(high_side, nz - 1, 0)
     inward = jnp.where(high_side, 1, 0)
-    up_ok = z <= nz - 3
-    down_ok = z >= 2
+    near = z - sgn
     unroll = max(u for u in range(1, 9) if rows % u == 0)
 
     barrier = pltpu.get_barrier_semaphore()
@@ -96,12 +97,6 @@
 
     lax.fori_loop(1, members, greet, 0)
     pl.semaphore_signal(barrier, inc=1, device_id={"col": 1 - col}, device_id_type=MESH)
-
-    @pl.when(is_end)
-    def _():
-        pl.semaphore_signal(
-            barrier, inc=1, device_id={"gx": z - sgn, "col": 1 - col}, device_id_type=MESH
-        )
 
     normed[pl.ds(rows * cols, LANES), :] = jnp.zeros((LANES, channels), bf16)
     step_rows = unroll
@@ -162,7 +157,7 @@
         return pltpu.make_async_remote_copy(
             src_ref=right_all.at[source, window],
             dst_ref=right_all.at[source, window],
-            send_sem=z_send.at[direction, source, c],
+            send_sem=z_send.at[direction, source],
             recv_sem=z_recv.at[source, c],
             device_id={"gx": toward},
             device_id_type=MESH,
@@ -173,13 +168,13 @@
         return pltpu.make_async_remote_copy(
             src_ref=left_t.at[window],
             dst_ref=left_r.at[window],
-            send_sem=l_send.at[c],
+            send_sem=l_send,
             recv_sem=l_recv.at[c],
-            device_id={"gx": z - sgn},
+            device_id={"gx": near},
             device_id_type=MESH,
         )
 
-    pl.semaphore_wait(barrier, members + jnp.where(is_next, 1, 0))
+    pl.semaphore_wait(barrier, members)
     early = chunks // 2
     for c in range(chunks):
         for g in range(2 * bounds[c], 2 * bounds[c + 1]):
@@ -187,11 +182,11 @@
             right_all[z, g] = tile[:cols].astype(bf16)
         now = True if c < early else jnp.logical_not(is_end)
 
-        @pl.when(up_ok & now)
+        @pl.when((z < nz - 1) & now)
         def _():
             z_copy(z, c, 0).start()
 
-        @pl.when(down_ok & now)
+        @pl.when((z > 0) & now)
         def _():
             z_copy(z, c, 1).start()
 
@@ -248,7 +243,7 @@
         return pltpu.make_async_remote_copy(
             src_ref=send_t.at[rowset, target, sub, window],
             dst_ref=recv_t.at[rowset, source, sub, window],
-            send_sem=x_send.at[rowset, target, sub, c],
+            send_sem=x_send.at[rowset, target, sub],
             recv_sem=x_recv.at[rowset, source, sub, c],
             device_id={"gy": target},
             device_id_type=MESH,
@@ -282,21 +277,6 @@
         return carry
 
     lax.fori_loop(0, rows // unroll, gate_step, 0)
-    ow_pad[...] = jnp.zeros_like(ow_pad)
-    stretch = ow_pad.shape[0] // 2
-    square = jnp.concatenate(
-        [out_weight_ref[...].astype(f32), jnp.zeros((LANES - half, channels), f32)], axis=0
-    )
-    turned = jnp.transpose(square)
-    for cc in range(2):
-        ow_pad[cc * stretch : cc * stretch + half, :] = turned[cc * half : (cc + 1) * half, :]
-    for s in range(per):
-        parts = [ow_pad[pl.ds(cc * stretch + s, slot, stride=per), :] for cc in range(2)]
-        parts.append(jnp.zeros((LANES - 2 * slot, LANES), f32))
-        back = jnp.transpose(jnp.concatenate(parts, axis=0))
-        mix_w[s * half : (s + 1) * half, :] = back[:half].astype(bf16)
-    spread_t[...] = jnp.zeros_like(spread_t)
-
     group_lane = lax.broadcasted_iota(jnp.int32, (1, LANES), 1)
 
     def lane_vector(scalar_of, g):
@@ -327,20 +307,20 @@
         return pltpu.make_async_remote_copy(
             src_ref=full_t.at[col, sub, window],
             dst_ref=full_t.at[col, sub, window],
-            send_sem=c_send.at[sub, c],
+            send_sem=c_send.at[sub],
             recv_sem=c_recv.at[sub, c],
             device_id={"col": 1 - col},
             device_id_type=MESH,
         )
 
-    def end_copy(sub, c, source, target):
+    def end_copy(sub, c):
         window = pl.ds(bounds[c], bounds[c + 1] - bounds[c])
         return pltpu.make_async_remote_copy(
             src_ref=ret_t.at[sub, window],
-            dst_ref=full_t.at[source, sub, window],
-            send_sem=e_send.at[target, sub, c],
-            recv_sem=e_recv.at[source, sub, c],
-            device_id={"gx": end, "col": target},
+            dst_ref=full_t.at[col, sub, window],
+            send_sem=e_send.at[sub],
+            recv_sem=e_recv.at[sub, c],
+            device_id={"gx": end},
             device_id_type=MESH,
         )
 
@@ -364,8 +344,7 @@
                 else:
                     full_t[col, sub, p] = result
             if rowset:
-                end_copy(sub, c, col, col).start()
-                end_copy(sub, c, col, 1 - col).start()
+                end_copy(sub, c).start()
             else:
                 c_copy(sub, c).start()
 
@@ -389,20 +368,8 @@
         return jnp.concatenate([result, result], axis=0)
 
     def norm_sub(sub):
-        r = y * ratio + sub
-        returned = is_end & (r != z)
-
-        @pl.when(returned)
-        def _():
-            for c in range(chunks):
-                for cc in range(2):
-                    end_copy(sub, c, cc, col).wait_recv()
-
-        @pl.when(jnp.logical_not(returned))
-        def _():
-            for c in range(chunks):
-                c_copy(sub, c).wait_recv()
-
+        for c in range(chunks):
+            c_copy(sub, c).wait_recv()
         total = jnp.zeros((2 * rows, LANES), f32)
         for p in range(pairs):
             total = total + full_t[0, sub, p].astype(f32) + full_t[1, sub, p].astype(f32)
@@ -419,18 +386,43 @@
             for cc in range(2):
                 t = (full_t[cc, sub, p].astype(f32) - mean) * factor
                 t = t * pair_vector(1 + cc, p) + pair_vector(3 + cc, p)
-                for u in range(2):
-                    at = (sub * 2 + cc) * slot + 2 * p + u
-                    spread_t[pl.ds(at, rows, stride=LANES), :] = t[u * rows : (u + 1) * rows]
+                for ch in range(2 * p * per, min(2 * (p + 1) * per, half)):
+                    u, s = ch // per - 2 * p, ch % per
+                    piece = t[u * rows : (u + 1) * rows]
+                    piece = pltpu.roll(piece, LANES - s * rows, 1) if s else piece
+                    at = sub * (rows * pitch) + cc * half + ch
+                    spread_t[pl.ds(at, rows, stride=pitch), :] = piece
 
     first_low = jnp.logical_xor(2 * y < ny, is_end)
     order = jnp.where(first_low, ratio - 1, 0)
     step_sign = jnp.where(first_low, -1, 1)
+
+    def norm_turn(turn):
+        norm_sub(order + step_sign * turn)
+
+    def return_block(r, c):
+        owner, sub = r // ratio, lax.rem(r, ratio)
+
+        @pl.when(owner == y)
+        def _():
+            end_copy(sub, c).wait_recv()
+            c_copy(sub, c).start()
 
     end_sequence = [("right", c) for c in range(early)] + [("left", c) for c in range(early)]
     for c in range(early, chunks):
         end_sequence += [("right", c), ("left", c)]
     within = nz == 4 and ratio == 2
+    returns, held, lefts = [], [], []
+    for s in range(2 * chunks):
+        kind, ce = end_sequence[s]
+        k, c = 1 + s // chunks, s % chunks
+        if kind == "left":
+            lefts.append(ce)
+        if c in lefts:
+            returns.append((k, c))
+        if kind == "left":
+            returns += [(kk, ce) for kk, cc in held if cc == ce]
+        held.append((k, c))
 
     @pl.when(is_next)
     def _():
@@ -444,7 +436,7 @@
                 z_copy(end, ce, inward).wait_recv()
                 z_copy(end, ce, inward).start()
             if within and s == 2 * chunks - 1:
-                norm_sub(order)
+                norm_turn(0)
             z_copy(source, c, 1 - inward).wait_recv()
             if kind == "left":
                 left_copy(ce).wait_recv()
@@ -459,7 +451,6 @@
             todo.append((0, source, c))
             if kind == "left":
                 todo += [(1, z - sgn * kk, ce) for kk, cc in held if cc == ce]
-                todo.append((1, z, ce))
             else:
                 todo.append((0, end, ce))
             held.append((k, c))
@@ -502,80 +493,94 @@
 
             lax.fori_loop(1, nz - 1, ring_step, 0)
 
-    if within:
-
-        @pl.when(is_end)
-        def _():
-            norm_sub(order)
-
-        norm_sub(order + step_sign)
-    else:
-        for t in range(ratio):
-            norm_sub(order + step_sign * t)
-
-    wide = lax.broadcasted_iota(jnp.int32, (half, LANES), 1)
-
-    def mix_one(i):
-        start = pl.multiple_of(i * LANES, LANES)
-        tile = spread_t[pl.ds(start, LANES), :].astype(bf16)
-        parts = [tile[rr * 2 * slot : (rr + 1) * 2 * slot] for rr in range(ratio)]
-        res = jnp.dot(
-            mix_w[:, 0 : 2 * slot], jnp.concatenate(parts, axis=1), preferred_element_type=f32
-        )
-        mixing = None
-        for rr in range(ratio):
-            total = None
-            for s in range(per):
-                piece = res[s * half : (s + 1) * half, rr * LANES : (rr + 1) * LANES]
-                shift = (rr - s) * rows % LANES
-                piece = pltpu.roll(piece, shift, 1) if shift else piece
-                total = piece if total is None else total + piece
-            mixing = total if mixing is None else jnp.where(wide >= rr * rows, total, mixing)
-        out_ref[i] = (gating[i] * mixing)[:, :cols].astype(bf16)
-
-    def mix_step(b, carry):
-        for u in range(unroll):
-            mix_one(b * unroll + u)
-        return carry
-
-    lax.fori_loop(0, rows // unroll, mix_step, 0)
+    @pl.when(is_end)
+    def _():
+        for c in range(chunks):
+            z_copy(near, c, 1 - inward).wait_recv()
+            triangle_block(0, near, c)
+            if c:
+                finish_block(0, near, c - 1)
+        finish_block(0, near, chunks - 1)
+        if within:
+
+            @pl.when((z // ratio == y))
+            def _():
+                norm_turn(0)
+
+        for k, c in returns:
+            return_block(near - sgn * k, c)
+
+        def farther_back(k, carry):
+            for c in range(chunks):
+                return_block(near - sgn * k, c)
+            return carry
+
+        if nz > 4:
+            lax.fori_loop(3, nz - 1, farther_back, 0)
+        if within:
+
+            @pl.when((z // ratio != y))
+            def _():
+                norm_turn(0)
+
+    for turn in range(1 if within else 0, ratio):
+        norm_turn(turn)
 
     others = peaks.at[pl.ds(0, members - 1)]
     pltpu.make_async_copy(others, others, peak_recv).wait()
     top = jnp.max(jnp.max(peaks[...], axis=0), axis=0, keepdims=True)
     amax_ref[0:1, :] = top[:, :half]
     amax_ref[1:2, :] = top[:, half:]
+    pltpu.make_async_copy(amax_ref, amax_hbm, amax_sem).start()
+
+    wide = lax.broadcasted_iota(jnp.int32, (half, LANES), 1)
+
+    def mix_step(b, carry):
+        for u in range(unroll):
+            i = b * unroll + u
+            tiles = [
+                spread_t[pl.ds((sub * rows + i) * pitch, channels), :].astype(bf16)
+                for sub in range(ratio)
+            ]
+            res = jnp.dot(
+                out_weight_ref[...], jnp.concatenate(tiles, axis=1), preferred_element_type=f32
+            )
+            mixing = res[:, :LANES]
+            for sub in range(1, ratio):
+                part = pltpu.roll(res[:, sub * LANES : (sub + 1) * LANES], sub * rows, 1)
+                mixing = jnp.where(wide >= sub * rows, part, mixing)
+            out_ref[i] = (gating[i] * mixing)[:, :cols].astype(bf16)
+        window = pl.ds(b * unroll, unroll)
+        pltpu.make_async_copy(out_ref.at[window], out_hbm.at[window], out_sem).start()
+        return carry
+
+    lax.fori_loop(0, rows // unroll, mix_step, 0)
 
     pltpu.make_async_copy(others, others, peak_send).wait()
+
+    def sent(ref, sem):
+        pltpu.make_async_copy(ref, ref, sem).wait()
 
     for sub in range(ratio):
         r = y * ratio + sub
-
-        @pl.when(jnp.logical_not(is_end) | (r == z))
+        sent(full_t.at[col, sub], c_send.at[sub])
+
+        @pl.when(is_next & (r != end) & (r != z))
         def _(sub=sub):
-            for c in range(chunks):
-                c_copy(sub, c).wait_send()
-
-        @pl.when(is_next & (r != end))
-        def _(sub=sub):
-            for c in range(chunks):
-                for target in range(2):
-                    end_copy(sub, c, col, target).wait_send()
+            sent(ret_t.at[sub], e_send.at[sub])
 
     def drain_x(t, carry):
         target = lax.rem(y + t, ny)
         for sub in range(ratio):
             r = target * ratio + sub
 
-            @pl.when(jnp.logical_not(is_end) | (r == z))
+            @pl.when(jnp.logical_not(is_end) | (r == z) | (r == near))
             def _(sub=sub):
-                for c in range(chunks):
-                    x_copy(0, target, sub, c, y).wait_send()
-
-            @pl.when(is_next & (r != end))
+                sent(send_t.at[0, target, sub], x_send.at[0, target, sub])
+
+            @pl.when(is_next & (r != end) & (r != z))
             def _(sub=sub):
-                for c in range(chunks):
-                    x_copy(1, target, sub, c, y).wait_send()
+                sent(send_t.at[1, target, sub], x_send.at[1, target, sub])
 
         return carry
 
@@ -583,23 +588,22 @@
 
     @pl.when(is_end)
     def _():
-        for c in range(chunks):
-            left_copy(c).wait_send()
+        sent(left_t, l_send)
 
     def drain_z(source, carry):
-        @pl.when((source <= z) & up_ok)
+        @pl.when((source <= z) & (z < nz - 1) & ((source == z) | (z <= nz - 3)))
         def _():
-            for c in range(chunks):
-                z_copy(source, c, 0).wait_send()
-
-        @pl.when((source >= z) & down_ok)
+            sent(right_all.at[source], z_send.at[0, source])
+
+        @pl.when((source >= z) & (z > 0) & ((source == z) | (z >= 2)))
         def _():
-            for c in range(chunks):
-                z_copy(source, c, 1).wait_send()
+            sent(right_all.at[source], z_send.at[1, source])
 
         return carry
 
     lax.fori_loop(0, nz, drain_z, 0)
+    pltpu.make_async_copy(amax_ref, amax_hbm, amax_sem).wait()
+    pltpu.make_async_copy(out_ref, out_hbm, out_sem).wait()
 
 
 def on_device(
@@ -623,13 +627,13 @@
     per = LANES // rows
     pairs = -(-half // (2 * per))
     groups = 2 * pairs
-    slot = LANES // (2 * ratio)
     members = nz * ny
     weights = jnp.transpose(proj_weight, (1, 2, 0)).reshape(4 * half, channels)
     scratch_rows = -(-((groups - 1) * per * rows + LANES) // 8) * 8
     dma = pltpu.SemaphoreType.DMA
     vmem = pl.BlockSpec(memory_space=pltpu.VMEM)
     smem = pl.BlockSpec(memory_space=pltpu.SMEM)
+    hbm = pl.BlockSpec(memory_space=pl.ANY)
     tile = (2 * rows, LANES)
     update, new_amax = pl.pallas_call(
         functools.partial(kernel, (nz, ny, rows, cols, half, chunks)),
@@ -638,7 +642,7 @@
             jax.ShapeDtypeStruct((2, half), f32),
         ),
         in_specs=[vmem, vmem, vmem, smem, vmem, vmem, vmem, vmem, smem, smem, vmem],
-        out_specs=(vmem, vmem),
+        out_specs=(hbm, hbm),
         scratch_shapes=[
             pltpu.VMEM((rows * cols + LANES, channels), bf16),
             pltpu.VMEM((rows, LANES), f32),
@@ -656,24 +660,26 @@
             pltpu.VMEM((2, ny, ratio, pairs) + tile, bf16),
             pltpu.VMEM((ratio, pairs) + tile, bf16),
             pltpu.VMEM((2, ratio, pairs) + tile, bf16),
-            pltpu.VMEM((rows * LANES, LANES), f32),
-            pltpu.VMEM((per * half, LANES), bf16),
-            pltpu.VMEM((2 * slot * per, LANES), f32),
+            pltpu.VMEM((ratio * rows * (channels + 1) + 8, LANES), f32),
+            pltpu.VMEM((rows, half, cols), bf16),
+            pltpu.VMEM((2, half), f32),
             pltpu.VMEM((5, groups, LANES), f32),
             pltpu.VMEM((rows, half, LANES), f32),
             pltpu.VMEM((members, 8, channels), f32),
             dma,
             dma,
-            dma((2, nz, chunks)),
+            dma((2, nz)),
             dma((nz, chunks)),
+            dma,
             dma((chunks,)),
-            dma((chunks,)),
+            dma((2, ny, ratio)),
             dma((2, ny, ratio, chunks)),
-            dma((2, ny, ratio, chunks)),
+            dma((ratio,)),
             dma((ratio, chunks)),
+            dma((ratio,)),
             dma((ratio, chunks)),
-            dma((2, ratio, chunks)),
-            dma((2, ratio, chunks)),
+            dma,
+            dma,
         ],
         compiler_params=pltpu.CompilerParams(
             collective_id=0, has_side_effects=True, vmem_limit_bytes=56 * 1024 * 1024

time: 51.1 us -> 47.3 us (0.926)
  Pallas kernels: 47.8 us -> 44 us
    pallas_call x1, Pallas kernels: 47.8 us -> 44 us  [on_device(): pl.pallas_call(functools.partial(kernel, (nz, ny, rows, cols, half, chunk...]
where the time goes in v2:
time: 47.3 us; the launch traced here: 47.2 us
  Pallas kernels  44 us (93%)
  local copies, waits for them, and re-layouts  2.53 us (5%)
  between operations  0.65 us (1%)
    pallas_call x1, Pallas kernels, on_device(): pl.pallas_call(functools.partial(kernel, (nz, ny, rows, cols, half, chunk...  44 us
    unnamed x4, local copies, waits for them, and re-layouts  2.53 us

profile of v2, /device:TPU:3, one launch (start us, length us, event | category | flops | bytes accessed | tf_op | source)
XLA Modules:
  0.0 47.2 jit_solution(8228715674530482820)
XLA Ops:
  0.6 44.0 %shard_map.113 = (bf16[40,64,80]{2,1,0:T(8,128)(2,1)}, f32[2,64]{1,0:T(2,128)}) custom-call(bf16[40,80,128]{2,1,0:T(8,128)(2,1)} %bitcast.12, s32[40,80]{1,0:T(8,128)} %bitcast.15, f32[2,64]{1,0:T(2,128)} %hist_smem.1, f32[2,64]{1,0:T(2,128)} %hist_smem.1, f32[1,128]{1,0:T(1,128)} %bitcast.18, f32[1,128]{1,0:T(1,128)} %bitcast.19, ...), custom_call_target="tpu_custom_call" | custom-call | tf_op jit(solution)/shard_map/pallas_call | solution.py:638
  44.6 0.0 copy-start
  44.6 2.0 %copy.14 = bf16[1,40,80,64]{2,3,1,0:T(8,128)(2,1)} copy(bf16[1,40,80,64]{2,3,1,0:T(8,128)(2,1)} %bitcast.13) | data formatting | bytes 819200
  46.6 0.0 copy-done
  46.6 0.6 %copy.15 = f32[2,64]{1,0:T(2,128)} copy(f32[2,64]{1,0:T(2,128)S(1)} %copy-done) | data formatting | bytes 1024
Async XLA Ops:
  44.6 2.0 %copy-start = (f32[2,64]{1,0:T(2,128)S(1)}, f32[2,64]{1,0:T(2,128)}, u32[]{:S(2)}) copy-start(f32[2,64]{1,0:T(2,128)} %get-tuple-element.9) | copy-start | bytes 1540

commit v3 on v2

--- a/solution.py
+++ b/solution.py
@@ -175,18 +175,16 @@
         )
 
     pl.semaphore_wait(barrier, members)
-    early = chunks // 2
     for c in range(chunks):
         for g in range(2 * bounds[c], 2 * bounds[c + 1]):
             tile = jnp.transpose(right_s[g * span : g * span + LANES, :])
             right_all[z, g] = tile[:cols].astype(bf16)
-        now = True if c < early else jnp.logical_not(is_end)
-
-        @pl.when((z < nz - 1) & now)
+
+        @pl.when(z < nz - 1)
         def _():
             z_copy(z, c, 0).start()
 
-        @pl.when((z > 0) & now)
+        @pl.when(z > 0)
         def _():
             z_copy(z, c, 1).start()
 
@@ -198,8 +196,6 @@
             for g in range(2 * bounds[c], 2 * bounds[c + 1]):
                 tile = jnp.transpose(left_s[g * span : g * span + LANES, :])
                 left_t[g] = tile[:cols].astype(bf16)
-            if c >= early:
-                z_copy(z, c, inward).start()
             left_copy(c).start()
 
     for g in range(groups):
@@ -347,9 +343,6 @@
                 end_copy(sub, c).start()
             else:
                 c_copy(sub, c).start()
-
-    for c in range(chunks):
-        finish_block(0, z, c)
 
     row_at = lax.broadcasted_iota(jnp.int32, (2 * rows, LANES), 0) // rows
     lane_at = lax.broadcasted_iota(jnp.int32, (2 * rows, LANES), 1) // rows
@@ -393,7 +386,7 @@
                     at = sub * (rows * pitch) + cc * half + ch
                     spread_t[pl.ds(at, rows, stride=pitch), :] = piece
 
-    first_low = jnp.logical_xor(2 * y < ny, is_end)
+    first_low = jnp.where(is_end, high_side, 2 * y < ny)
     order = jnp.where(first_low, ratio - 1, 0)
     step_sign = jnp.where(first_low, -1, 1)
 
@@ -408,59 +401,41 @@
             end_copy(sub, c).wait_recv()
             c_copy(sub, c).start()
 
-    end_sequence = [("right", c) for c in range(early)] + [("left", c) for c in range(early)]
-    for c in range(early, chunks):
-        end_sequence += [("right", c), ("left", c)]
     within = nz == 4 and ratio == 2
-    returns, held, lefts = [], [], []
-    for s in range(2 * chunks):
-        kind, ce = end_sequence[s]
-        k, c = 1 + s // chunks, s % chunks
-        if kind == "left":
-            lefts.append(ce)
-        if c in lefts:
-            returns.append((k, c))
-        if kind == "left":
-            returns += [(kk, ce) for kk, cc in held if cc == ce]
-        held.append((k, c))
+    second = near - sgn
 
     @pl.when(is_next)
     def _():
-        lefts, held, pending = [], [], []
+        queue = [[(0, z, c) for c in range(chunks)]]
         for s in range(2 * chunks):
-            kind, ce = end_sequence[s]
             k, c = 1 + s // chunks, s % chunks
             source = z - sgn * k
-            todo = []
-            if kind == "right":
-                z_copy(end, ce, inward).wait_recv()
-                z_copy(end, ce, inward).start()
-            if within and s == 2 * chunks - 1:
+            if k == 1:
+                z_copy(end, c, inward).wait_recv()
+                z_copy(end, c, inward).start()
+            elif within and c == chunks - 1:
                 norm_turn(0)
             z_copy(source, c, 1 - inward).wait_recv()
-            if kind == "left":
-                left_copy(ce).wait_recv()
-                for g in range(2 * bounds[ce], 2 * bounds[ce + 1]):
+            if k == 1:
+                z_copy(source, c, 1 - inward).start()
+                todo = [(0, source, c), (0, end, c)]
+            else:
+                left_copy(c).wait_recv()
+                for g in range(2 * bounds[c], 2 * bounds[c + 1]):
                     tile = jnp.concatenate(
                         [left_r[g].astype(f32), jnp.zeros((LANES - cols, LANES), f32)], axis=0
                     )
                     left_e[g] = jnp.transpose(tile).astype(bf16)
-                lefts.append(ce)
-            if c in lefts:
-                todo.append((1, source, c))
-            todo.append((0, source, c))
-            if kind == "left":
-                todo += [(1, z - sgn * kk, ce) for kk, cc in held if cc == ce]
-            else:
-                todo.append((0, end, ce))
-            held.append((k, c))
+                todo = [(1, source, c), (0, source, c)]
             for block in todo:
                 triangle_block(*block)
-            for block in pending:
+            queue.append(todo)
+            if s >= 2:
+                for block in queue.pop(0):
+                    finish_block(*block)
+        for todo in queue:
+            for block in todo:
                 finish_block(*block)
-            pending = todo
-        for block in pending:
-            finish_block(*block)
 
         def farther(k, carry):
             for c in range(chunks):
@@ -492,36 +467,43 @@
                 return carry
 
             lax.fori_loop(1, nz - 1, ring_step, 0)
+            for c in range(chunks):
+                finish_block(0, z, c)
 
     @pl.when(is_end)
     def _():
+        def arrived(source, c):
+            z_copy(source, c, 1 - inward).wait_recv()
+            triangle_block(0, source, c)
+
+        def norm_if(here):
+            if within:
+
+                @pl.when(here)
+                def _():
+                    norm_turn(0)
+
         for c in range(chunks):
-            z_copy(near, c, 1 - inward).wait_recv()
-            triangle_block(0, near, c)
-            if c:
-                finish_block(0, near, c - 1)
-        finish_block(0, near, chunks - 1)
-        if within:
-
-            @pl.when((z // ratio == y))
-            def _():
-                norm_turn(0)
-
-        for k, c in returns:
-            return_block(near - sgn * k, c)
+            arrived(near, c)
+        for c in range(chunks):
+            finish_block(0, z, c)
+        arrived(second, 0)
+        for c in range(chunks):
+            finish_block(0, near, c)
+        for c in range(1, chunks):
+            if c == chunks // 2:
+                norm_if(z // ratio == y)
+            arrived(second, c)
+            finish_block(0, second, c - 1)
+        finish_block(0, second, chunks - 1)
+        norm_if(z // ratio != y)
 
         def farther_back(k, carry):
             for c in range(chunks):
                 return_block(near - sgn * k, c)
             return carry
 
-        if nz > 4:
-            lax.fori_loop(3, nz - 1, farther_back, 0)
-        if within:
-
-            @pl.when((z // ratio != y))
-            def _():
-                norm_turn(0)
+        lax.fori_loop(2, nz - 1, farther_back, 0)
 
     for turn in range(1 if within else 0, ratio):
         norm_turn(turn)
@@ -565,7 +547,7 @@
         r = y * ratio + sub
         sent(full_t.at[col, sub], c_send.at[sub])
 
-        @pl.when(is_next & (r != end) & (r != z))
+        @pl.when(is_next & (r != end) & (r != z) & (r != near))
         def _(sub=sub):
             sent(ret_t.at[sub], e_send.at[sub])
 
@@ -574,11 +556,11 @@
         for sub in range(ratio):
             r = target * ratio + sub
 
-            @pl.when(jnp.logical_not(is_end) | (r == z) | (r == near))
+            @pl.when(jnp.logical_not(is_end) | (r == z) | (r == near) | (r == second))
             def _(sub=sub):
                 sent(send_t.at[0, target, sub], x_send.at[0, target, sub])
 
-            @pl.when(is_next & (r != end) & (r != z))
+            @pl.when(is_next & (r != end) & (r != z) & (r != near))
             def _(sub=sub):
                 sent(send_t.at[1, target, sub], x_send.at[1, target, sub])
 
@@ -591,11 +573,11 @@
         sent(left_t, l_send)
 
     def drain_z(source, carry):
-        @pl.when((source <= z) & (z < nz - 1) & ((source == z) | (z <= nz - 3)))
+        @pl.when((source <= z) & (z < nz - 1) & ((source >= z - 1) | (z <= nz - 3)))
         def _():
             sent(right_all.at[source], z_send.at[0, source])
 
-        @pl.when((source >= z) & (z > 0) & ((source == z) | (z >= 2)))
+        @pl.when((source >= z) & (z > 0) & ((source <= z + 1) | (z >= 2)))
         def _():
             sent(right_all.at[source], z_send.at[1, source])
 

time: 47.3 us -> 43.9 us (0.928)
  Pallas kernels: 44 us -> 40.5 us
    pallas_call x1, Pallas kernels: 44 us -> 40.5 us  [on_device(): pl.pallas_call(functools.partial(kernel, (nz, ny, rows, cols, half, chunk...]
where the time goes in v3:
time: 43.9 us; the launch traced here: 43.7 us
  Pallas kernels  40.5 us (92%)
  local copies, waits for them, and re-layouts  2.53 us (6%)
  between operations  0.65 us (1%)
    pallas_call x1, Pallas kernels, on_device(): pl.pallas_call(functools.partial(kernel, (nz, ny, rows, cols, half, chunk...  40.5 us
    unnamed x4, local copies, waits for them, and re-layouts  2.53 us

profile of v3, /device:TPU:3, one launch (start us, length us, event | category | flops | bytes accessed | tf_op | source)
XLA Modules:
  0.0 43.7 jit_solution(11296486460392319118)
XLA Ops:
  0.6 40.5 %shard_map.113 = (bf16[40,64,80]{2,1,0:T(8,128)(2,1)}, f32[2,64]{1,0:T(2,128)}) custom-call(bf16[40,80,128]{2,1,0:T(8,128)(2,1)} %bitcast.12, s32[40,80]{1,0:T(8,128)} %bitcast.15, f32[2,64]{1,0:T(2,128)} %hist_smem.1, f32[2,64]{1,0:T(2,128)} %hist_smem.1, f32[1,128]{1,0:T(1,128)} %bitcast.18, f32[1,128]{1,0:T(1,128)} %bitcast.19, ...), custom_call_target="tpu_custom_call" | custom-call | tf_op jit(solution)/shard_map/pallas_call | solution.py:620
  41.2 0.0 copy-start
  41.2 2.0 %copy.14 = bf16[1,40,80,64]{2,3,1,0:T(8,128)(2,1)} copy(bf16[1,40,80,64]{2,3,1,0:T(8,128)(2,1)} %bitcast.13) | data formatting | bytes 819200
  43.2 0.0 copy-done
  43.2 0.6 %copy.15 = f32[2,64]{1,0:T(2,128)} copy(f32[2,64]{1,0:T(2,128)S(1)} %copy-done) | data formatting | bytes 1024
Async XLA Ops:
  41.2 2.0 %copy-start = (f32[2,64]{1,0:T(2,128)S(1)}, f32[2,64]{1,0:T(2,128)}, u32[]{:S(2)}) copy-start(f32[2,64]{1,0:T(2,128)} %get-tuple-element.9) | copy-start | bytes 1540

commit v4 on v3

--- a/solution.py
+++ b/solution.py
@@ -27,8 +27,8 @@
     out_gain_smem,
     out_bias_smem,
     out_weight_ref,
-    out_hbm,
-    amax_hbm,
+    out_ref,
+    amax_ref,
     normed,
     maskf,
     inverse,
@@ -46,8 +46,6 @@
     ret_t,
     full_t,
     spread_t,
-    out_ref,
-    amax_ref,
     vecs,
     gating,
     peaks,
@@ -63,8 +61,6 @@
     c_recv,
     e_send,
     e_recv,
-    out_sem,
-    amax_sem,
 ):
     nz, ny, rows, cols, half, chunks = dims
     ratio = nz // ny
@@ -149,7 +145,7 @@
         peak[base : base + half, :] = top
 
     project(1, right_s)
-    bounds = [pairs * c // chunks for c in range(chunks + 1)]
+    bounds = [-(-pairs * c // chunks) for c in range(chunks + 1)]
 
     def z_copy(source, c, direction):
         window = pl.ds(2 * bounds[c], 2 * (bounds[c + 1] - bounds[c]))
@@ -433,6 +429,9 @@
             if s >= 2:
                 for block in queue.pop(0):
                     finish_block(*block)
+            if s >= chunks and len(queue) > 2:
+                for block in queue.pop(0):
+                    finish_block(*block)
         for todo in queue:
             for block in todo:
                 finish_block(*block)
@@ -513,7 +512,6 @@
     top = jnp.max(jnp.max(peaks[...], axis=0), axis=0, keepdims=True)
     amax_ref[0:1, :] = top[:, :half]
     amax_ref[1:2, :] = top[:, half:]
-    pltpu.make_async_copy(amax_ref, amax_hbm, amax_sem).start()
 
     wide = lax.broadcasted_iota(jnp.int32, (half, LANES), 1)
 
@@ -532,8 +530,6 @@
                 part = pltpu.roll(res[:, sub * LANES : (sub + 1) * LANES], sub * rows, 1)
                 mixing = jnp.where(wide >= sub * rows, part, mixing)
             out_ref[i] = (gating[i] * mixing)[:, :cols].astype(bf16)
-        window = pl.ds(b * unroll, unroll)
-        pltpu.make_async_copy(out_ref.at[window], out_hbm.at[window], out_sem).start()
         return carry
 
     lax.fori_loop(0, rows // unroll, mix_step, 0)
@@ -584,8 +580,6 @@
         return carry
 
     lax.fori_loop(0, nz, drain_z, 0)
-    pltpu.make_async_copy(amax_ref, amax_hbm, amax_sem).wait()
-    pltpu.make_async_copy(out_ref, out_hbm, out_sem).wait()
 
 
 def on_device(
@@ -604,7 +598,7 @@
 ):
     crops, rows, cols, channels = pair_rep.shape
     half = proj_weight.shape[2]
-    chunks = 4
+    chunks = 5
     ratio = nz // ny
     per = LANES // rows
     pairs = -(-half // (2 * per))
@@ -615,16 +609,15 @@
     dma = pltpu.SemaphoreType.DMA
     vmem = pl.BlockSpec(memory_space=pltpu.VMEM)
     smem = pl.BlockSpec(memory_space=pltpu.SMEM)
-    hbm = pl.BlockSpec(memory_space=pl.ANY)
     tile = (2 * rows, LANES)
     update, new_amax = pl.pallas_call(
         functools.partial(kernel, (nz, ny, rows, cols, half, chunks)),
         out_shape=(
-            jax.ShapeDtypeStruct((rows, half, cols), bf16),
-            jax.ShapeDtypeStruct((2, half), f32),
+            pltpu.VMEM((rows, half, cols), bf16),
+            pltpu.VMEM((2, half), f32),
         ),
         in_specs=[vmem, vmem, vmem, smem, vmem, vmem, vmem, vmem, smem, smem, vmem],
-        out_specs=(hbm, hbm),
+        out_specs=(vmem, vmem),
         scratch_shapes=[
             pltpu.VMEM((rows * cols + LANES, channels), bf16),
             pltpu.VMEM((rows, LANES), f32),
@@ -643,8 +636,6 @@
             pltpu.VMEM((ratio, pairs) + tile, bf16),
             pltpu.VMEM((2, ratio, pairs) + tile, bf16),
             pltpu.VMEM((ratio * rows * (channels + 1) + 8, LANES), f32),
-            pltpu.VMEM((rows, half, cols), bf16),
-            pltpu.VMEM((2, half), f32),
             pltpu.VMEM((5, groups, LANES), f32),
             pltpu.VMEM((rows, half, LANES), f32),
             pltpu.VMEM((members, 8, channels), f32),
@@ -660,8 +651,6 @@
             dma((ratio, chunks)),
             dma((ratio,)),
             dma((ratio, chunks)),
-            dma,
-            dma,
         ],
         compiler_params=pltpu.CompilerParams(
             collective_id=0, has_side_effects=True, vmem_limit_bytes=56 * 1024 * 1024

time: 43.9 us -> 41.1 us (0.936)
  Pallas kernels: 40.5 us -> 38.9 us
  local copies, waits for them, and re-layouts: 2.53 us -> 1.4 us
    pallas_call x1, Pallas kernels: 40.5 us -> 38.9 us  [on_device(): pl.pallas_call(functools.partial(kernel, (nz, ny, rows, cols, half, chunk...]
    unnamed x4 -> x2, local copies, waits for them, and re-layouts: 2.53 us -> 1.4 us
where the time goes in v4:
time: 41.1 us; the launch traced here: 40.9 us
  Pallas kernels  38.9 us (95%)
  local copies, waits for them, and re-layouts  1.4 us (3%)
  between operations  0.64 us (2%)
    pallas_call x1, Pallas kernels, on_device(): pl.pallas_call(functools.partial(kernel, (nz, ny, rows, cols, half, chunk...  38.9 us
    unnamed x2, local copies, waits for them, and re-layouts  1.4 us

profile of v4, /device:TPU:3, one launch (start us, length us, event | category | flops | bytes accessed | tf_op | source)
XLA Modules:
  0.0 40.9 jit_solution(17551687827533397689)
XLA Ops:
  0.6 38.9 %shard_map.113 = (bf16[40,64,80]{2,1,0:T(8,128)(2,1)S(1)}, f32[2,64]{1,0:T(2,128)S(1)}) custom-call(bf16[40,80,128]{2,1,0:T(8,128)(2,1)} %bitcast.13, s32[40,80]{1,0:T(8,128)} %bitcast.15, f32[2,64]{1,0:T(2,128)} %hist_smem.1, f32[2,64]{1,0:T(2,128)} %hist_smem.1, f32[1,128]{1,0:T(1,128)} %bitcast.18, f32[1,128]{1,0:T(1,128)} %bitcast.19, ...), custom_call_target="tpu_custom_call" | custom-call | tf_op jit(solution)/shard_map/pallas_call | solution.py:613
  39.5 0.8 %copy.14 = bf16[1,40,80,64]{2,3,1,0:T(8,128)(2,1)} copy(bf16[1,40,80,64]{2,3,1,0:T(8,128)(2,1)S(1)} %bitcast.12) | data formatting | bytes 819200
  40.4 0.6 %copy.15 = f32[2,64]{1,0:T(2,128)} copy(f32[2,64]{1,0:T(2,128)S(1)} %get-tuple-element.7) | data formatting | bytes 1024

commit v5 on v4

--- a/solution.py
+++ b/solution.py
@@ -47,6 +47,7 @@
     full_t,
     spread_t,
     vecs,
+    mixed,
     gating,
     peaks,
     peak_send,
@@ -80,7 +81,11 @@
     end = jnp.where(high_side, nz - 1, 0)
     inward = jnp.where(high_side, 1, 0)
     near = z - sgn
-    unroll = max(u for u in range(1, 9) if rows % u == 0)
+
+    def steps(limit):
+        return max(u for u in range(1, limit + 1) if rows % u == 0)
+
+    step_rows, project_rows, gate_rows, mix_rows = steps(40), steps(40), steps(40), steps(40)
 
     barrier = pltpu.get_barrier_semaphore()
 
@@ -95,12 +100,13 @@
     pl.semaphore_signal(barrier, inc=1, device_id={"col": 1 - col}, device_id_type=MESH)
 
     normed[pl.ds(rows * cols, LANES), :] = jnp.zeros((LANES, channels), bf16)
-    step_rows = unroll
+
+    ones = jnp.ones((channels, channels), bf16)
 
     def norm_step(b, carry):
-        values = rep_ref[pl.ds(b * step_rows, step_rows)].reshape(step_rows * cols, channels).astype(f32)
-        average = jnp.mean(values, axis=-1, keepdims=True)
-        centred = values - average
+        values = rep_ref[pl.ds(b * step_rows, step_rows)].reshape(step_rows * cols, channels)
+        average = jnp.dot(values, ones, preferred_element_type=f32) * (1.0 / channels)
+        centred = values.astype(f32) - average
         var = jnp.mean(jnp.square(centred), axis=-1, keepdims=True)
         result = centred * lax.rsqrt(var + epsilon) * in_gain_ref[...] + in_bias_ref[...]
         start = pl.multiple_of(b * step_rows * cols, 16)
@@ -137,11 +143,11 @@
             return jnp.abs(value)
 
         def step(b, top):
-            for u in range(unroll):
-                top = jnp.maximum(top, one(b * unroll + u))
+            for u in range(project_rows):
+                top = jnp.maximum(top, one(b * project_rows + u))
             return top
 
-        top = lax.fori_loop(0, rows // unroll, step, jnp.zeros((half, LANES), f32))
+        top = lax.fori_loop(0, rows // project_rows, step, jnp.zeros((half, LANES), f32))
         peak[base : base + half, :] = top
 
     project(1, right_s)
@@ -258,8 +264,8 @@
         triangle_block(0, z, c)
 
     def gate_step(b, carry):
-        for u in range(unroll):
-            i = b * unroll + u
+        for u in range(gate_rows):
+            i = b * gate_rows + u
             block = normed[pl.ds(pl.multiple_of(i * cols, 16), LANES), :]
             gating[i] = jax.nn.sigmoid(
                 lax.dot_general(
@@ -268,7 +274,7 @@
             )
         return carry
 
-    lax.fori_loop(0, rows // unroll, gate_step, 0)
+    lax.fori_loop(0, rows // gate_rows, gate_step, 0)
     group_lane = lax.broadcasted_iota(jnp.int32, (1, LANES), 1)
 
     def lane_vector(scalar_of, g):
@@ -389,6 +395,28 @@
     def norm_turn(turn):
         norm_sub(order + step_sign * turn)
 
+    wide = lax.broadcasted_iota(jnp.int32, (half, LANES), 1)
+
+    def mix_turn(turn):
+        sub = order + step_sign * turn
+        inside = (wide >= sub * rows) & (wide < (sub + 1) * rows)
+
+        def mix_step(b, carry):
+            for u in range(mix_rows):
+                i = b * mix_rows + u
+                tile = spread_t[pl.ds((sub * rows + i) * pitch, channels), :].astype(bf16)
+                mixing = jnp.dot(out_weight_ref[...], tile, preferred_element_type=f32)
+                mixing = pltpu.roll(mixing, sub * rows, 1)
+                if turn:
+                    mixing = jnp.where(inside, mixing, mixed[i])
+                if turn < ratio - 1:
+                    mixed[i] = mixing
+                else:
+                    out_ref[i] = (gating[i] * mixing)[:, :cols].astype(bf16)
+            return carry
+
+        lax.fori_loop(0, rows // mix_rows, mix_step, 0)
+
     def return_block(r, c):
         owner, sub = r // ratio, lax.rem(r, ratio)
 
@@ -409,8 +437,6 @@
             if k == 1:
                 z_copy(end, c, inward).wait_recv()
                 z_copy(end, c, inward).start()
-            elif within and c == chunks - 1:
-                norm_turn(0)
             z_copy(source, c, 1 - inward).wait_recv()
             if k == 1:
                 z_copy(source, c, 1 - inward).start()
@@ -432,9 +458,13 @@
             if s >= chunks and len(queue) > 2:
                 for block in queue.pop(0):
                     finish_block(*block)
+        if within:
+            norm_turn(0)
         for todo in queue:
             for block in todo:
                 finish_block(*block)
+        if within:
+            mix_turn(0)
 
         def farther(k, carry):
             for c in range(chunks):
@@ -496,6 +526,8 @@
             finish_block(0, second, c - 1)
         finish_block(0, second, chunks - 1)
         norm_if(z // ratio != y)
+        if within:
+            mix_turn(0)
 
         def farther_back(k, carry):
             for c in range(chunks):
@@ -503,9 +535,6 @@
             return carry
 
         lax.fori_loop(2, nz - 1, farther_back, 0)
-
-    for turn in range(1 if within else 0, ratio):
-        norm_turn(turn)
 
     others = peaks.at[pl.ds(0, members - 1)]
     pltpu.make_async_copy(others, others, peak_recv).wait()
@@ -513,39 +542,10 @@
     amax_ref[0:1, :] = top[:, :half]
     amax_ref[1:2, :] = top[:, half:]
 
-    wide = lax.broadcasted_iota(jnp.int32, (half, LANES), 1)
-
-    def mix_step(b, carry):
-        for u in range(unroll):
-            i = b * unroll + u
-            tiles = [
-                spread_t[pl.ds((sub * rows + i) * pitch, channels), :].astype(bf16)
-                for sub in range(ratio)
-            ]
-            res = jnp.dot(
-                out_weight_ref[...], jnp.concatenate(tiles, axis=1), preferred_element_type=f32
-            )
-            mixing = res[:, :LANES]
-            for sub in range(1, ratio):
-                part = pltpu.roll(res[:, sub * LANES : (sub + 1) * LANES], sub * rows, 1)
-                mixing = jnp.where(wide >= sub * rows, part, mixing)
-            out_ref[i] = (gating[i] * mixing)[:, :cols].astype(bf16)
-        return carry
-
-    lax.fori_loop(0, rows // unroll, mix_step, 0)
-
     pltpu.make_async_copy(others, others, peak_send).wait()
 
     def sent(ref, sem):
         pltpu.make_async_copy(ref, ref, sem).wait()
-
-    for sub in range(ratio):
-        r = y * ratio + sub
-        sent(full_t.at[col, sub], c_send.at[sub])
-
-        @pl.when(is_next & (r != end) & (r != z) & (r != near))
-        def _(sub=sub):
-            sent(ret_t.at[sub], e_send.at[sub])
 
     def drain_x(t, carry):
         target = lax.rem(y + t, ny)
@@ -580,6 +580,18 @@
         return carry
 
     lax.fori_loop(0, nz, drain_z, 0)
+
+    for turn in range(1 if within else 0, ratio):
+        norm_turn(turn)
+        mix_turn(turn)
+
+    for sub in range(ratio):
+        r = y * ratio + sub
+        sent(full_t.at[col, sub], c_send.at[sub])
+
+        @pl.when(is_next & (r != end) & (r != z) & (r != near))
+        def _(sub=sub):
+            sent(ret_t.at[sub], e_send.at[sub])
 
 
 def on_device(
@@ -638,6 +650,7 @@
             pltpu.VMEM((ratio * rows * (channels + 1) + 8, LANES), f32),
             pltpu.VMEM((5, groups, LANES), f32),
             pltpu.VMEM((rows, half, LANES), f32),
+            pltpu.VMEM((rows, half, LANES), f32),
             pltpu.VMEM((members, 8, channels), f32),
             dma,
             dma,

time: 41.1 us -> 39.4 us (0.959)
  Pallas kernels: 38.9 us -> 37.2 us
    pallas_call x1, Pallas kernels: 38.9 us -> 37.2 us  [on_device(): pl.pallas_call(functools.partial(kernel, (nz, ny, rows, cols, half, chunk...]
where the time goes in v5:
time: 39.4 us; the launch traced here: 39.2 us
  Pallas kernels  37.2 us (94%)
  local copies, waits for them, and re-layouts  1.4 us (4%)
  between operations  0.64 us (2%)
    pallas_call x1, Pallas kernels, on_device(): pl.pallas_call(functools.partial(kernel, (nz, ny, rows, cols, half, chunk...  37.2 us
    unnamed x2, local copies, waits for them, and re-layouts  1.4 us

profile of v5, /device:TPU:3, one launch (start us, length us, event | category | flops | bytes accessed | tf_op | source)
XLA Modules:
  0.0 39.2 jit_solution(10623517399332920367)
XLA Ops:
  0.6 37.2 %shard_map.113 = (bf16[40,64,80]{2,1,0:T(8,128)(2,1)S(1)}, f32[2,64]{1,0:T(2,128)S(1)}) custom-call(bf16[40,80,128]{2,1,0:T(8,128)(2,1)} %bitcast.13, s32[40,80]{1,0:T(8,128)} %bitcast.15, f32[2,64]{1,0:T(2,128)} %hist_smem.1, f32[2,64]{1,0:T(2,128)} %hist_smem.1, f32[1,128]{1,0:T(1,128)} %bitcast.18, f32[1,128]{1,0:T(1,128)} %bitcast.19, ...), custom_call_target="tpu_custom_call" | custom-call | tf_op jit(solution)/shard_map/pallas_call | solution.py:625
  37.8 0.8 %copy.14 = bf16[1,40,80,64]{2,3,1,0:T(8,128)(2,1)} copy(bf16[1,40,80,64]{2,3,1,0:T(8,128)(2,1)S(1)} %bitcast.12) | data formatting | bytes 819200
  38.7 0.6 %copy.15 = f32[2,64]{1,0:T(2,128)} copy(f32[2,64]{1,0:T(2,128)S(1)} %get-tuple-element.7) | data formatting | bytes 1024

commit v6 on v5

--- a/solution.py
+++ b/solution.py
@@ -43,7 +43,6 @@
     own_t,
     send_t,
     recv_t,
-    ret_t,
     full_t,
     spread_t,
     vecs,
@@ -60,8 +59,6 @@
     x_recv,
     c_send,
     c_recv,
-    e_send,
-    e_recv,
 ):
     nz, ny, rows, cols, half, chunks = dims
     ratio = nz // ny
@@ -182,11 +179,13 @@
             tile = jnp.transpose(right_s[g * span : g * span + LANES, :])
             right_all[z, g] = tile[:cols].astype(bf16)
 
-        @pl.when(z < nz - 1)
+        now = True if c < 2 else jnp.logical_not(is_end)
+
+        @pl.when((z < nz - 1) & now)
         def _():
             z_copy(z, c, 0).start()
 
-        @pl.when(z > 0)
+        @pl.when((z > 0) & now)
         def _():
             z_copy(z, c, 1).start()
 
@@ -199,6 +198,8 @@
                 tile = jnp.transpose(left_s[g * span : g * span + LANES, :])
                 left_t[g] = tile[:cols].astype(bf16)
             left_copy(c).start()
+            if c + 2 < chunks:
+                z_copy(z, c + 2, inward).start()
 
     for g in range(groups):
         left_b[g] = left_s[g * span : g * span + LANES, :].astype(bf16)
@@ -236,32 +237,48 @@
             halves.append(t)
         return jnp.concatenate(halves, axis=0)
 
-    def x_copy(rowset, target, sub, c, source):
+    def x_copy(target, sub, c, source):
         window = pl.ds(bounds[c], bounds[c + 1] - bounds[c])
         return pltpu.make_async_remote_copy(
-            src_ref=send_t.at[rowset, target, sub, window],
-            dst_ref=recv_t.at[rowset, source, sub, window],
-            send_sem=x_send.at[rowset, target, sub],
-            recv_sem=x_recv.at[rowset, source, sub, c],
+            src_ref=send_t.at[0, target, sub, window],
+            dst_ref=recv_t.at[0, source, sub, window],
+            send_sem=x_send.at[0, target, sub],
+            recv_sem=x_recv.at[0, source, sub, c],
             device_id={"gy": target},
             device_id_type=MESH,
         )
 
-    def triangle_block(rowset, r, c):
+    def far_copy(owner, sub, c, source):
+        window = pl.ds(bounds[c], bounds[c + 1] - bounds[c])
+        return pltpu.make_async_remote_copy(
+            src_ref=send_t.at[1, owner, sub, window],
+            dst_ref=recv_t.at[1, source, sub, window],
+            send_sem=x_send.at[1, owner, sub],
+            recv_sem=x_recv.at[1, source, sub, c],
+            device_id={"gx": end, "gy": owner},
+            device_id_type=MESH,
+        )
+
+    def triangle_block(r, c):
         owner, sub = r // ratio, lax.rem(r, ratio)
         slot = jnp.where(owner == y, sub, ratio)
-        lhs = left_e if rowset else left_b
         for p in range(bounds[c], bounds[c + 1]):
-            t = triangle_pair(lhs, r, p)
-            own_t[rowset, slot, p] = t
-            send_t[rowset, owner, sub, p] = t.astype(bf16)
+            t = triangle_pair(left_b, r, p)
+            own_t[slot, p] = t
+            send_t[0, owner, sub, p] = t.astype(bf16)
 
         @pl.when(owner != y)
         def _():
-            x_copy(rowset, owner, sub, c, y).start()
+            x_copy(owner, sub, c, y).start()
+
+    def far_block(r, c):
+        owner, sub = r // ratio, lax.rem(r, ratio)
+        for p in range(bounds[c], bounds[c + 1]):
+            send_t[1, owner, sub, p] = triangle_pair(left_e, r, p).astype(bf16)
+        far_copy(owner, sub, c, y).start()
 
     for c in range(chunks):
-        triangle_block(0, z, c)
+        triangle_block(z, c)
 
     def gate_step(b, carry):
         for u in range(gate_rows):
@@ -311,40 +328,22 @@
             device_id_type=MESH,
         )
 
-    def end_copy(sub, c):
-        window = pl.ds(bounds[c], bounds[c + 1] - bounds[c])
-        return pltpu.make_async_remote_copy(
-            src_ref=ret_t.at[sub, window],
-            dst_ref=full_t.at[col, sub, window],
-            send_sem=e_send.at[sub],
-            recv_sem=e_recv.at[sub, c],
-            device_id={"gx": end},
-            device_id_type=MESH,
-        )
-
-    def finish_block(rowset, r, c):
+    def finish_block(r, c):
         owner, sub = r // ratio, lax.rem(r, ratio)
 
         @pl.when(owner == y)
         def _():
             def arrive(t, carry):
-                x_copy(rowset, y, sub, c, lax.rem(y + t, ny)).wait_recv()
+                x_copy(y, sub, c, lax.rem(y + t, ny)).wait_recv()
                 return carry
 
             lax.fori_loop(1, ny, arrive, 0)
             for p in range(bounds[c], bounds[c + 1]):
-                total = own_t[rowset, sub, p]
+                total = own_t[sub, p]
                 for t in range(1, ny):
-                    total = total + recv_t[rowset, lax.rem(y + t, ny), sub, p].astype(f32)
-                result = (total * pair_vector(0, p)).astype(bf16)
-                if rowset:
-                    ret_t[sub, p] = result
-                else:
-                    full_t[col, sub, p] = result
-            if rowset:
-                end_copy(sub, c).start()
-            else:
-                c_copy(sub, c).start()
+                    total = total + recv_t[0, lax.rem(y + t, ny), sub, p].astype(f32)
+                full_t[col, sub, p] = (total * pair_vector(0, p)).astype(bf16)
+            c_copy(sub, c).start()
 
     row_at = lax.broadcasted_iota(jnp.int32, (2 * rows, LANES), 0) // rows
     lane_at = lax.broadcasted_iota(jnp.int32, (2 * rows, LANES), 1) // rows
@@ -422,33 +421,53 @@
 
         @pl.when(owner == y)
         def _():
-            end_copy(sub, c).wait_recv()
+            def arrive(source, carry):
+                far_copy(y, sub, c, source).wait_recv()
+                return carry
+
+            lax.fori_loop(0, ny, arrive, 0)
+            for p in range(bounds[c], bounds[c + 1]):
+                total = recv_t[1, 0, sub, p].astype(f32)
+                for source in range(1, ny):
+                    total = total + recv_t[1, source, sub, p].astype(f32)
+                full_t[col, sub, p] = (total * pair_vector(0, p)).astype(bf16)
             c_copy(sub, c).start()
 
     within = nz == 4 and ratio == 2
-    second = near - sgn
 
     @pl.when(is_next)
     def _():
-        queue = [[(0, z, c) for c in range(chunks)]]
+        end_order = [("right", c) for c in range(min(2, chunks))]
+        for c in range(chunks):
+            end_order.append(("left", c))
+            if c + 2 < chunks:
+                end_order.append(("right", c + 2))
+        queue = [[(z, c) for c in range(chunks)]]
+        held, lefts = [], []
         for s in range(2 * chunks):
+            kind, ce = end_order[s]
             k, c = 1 + s // chunks, s % chunks
             source = z - sgn * k
-            if k == 1:
-                z_copy(end, c, inward).wait_recv()
-                z_copy(end, c, inward).start()
+            if kind == "right":
+                z_copy(end, ce, inward).wait_recv()
+                z_copy(end, ce, inward).start()
             z_copy(source, c, 1 - inward).wait_recv()
-            if k == 1:
-                z_copy(source, c, 1 - inward).start()
-                todo = [(0, source, c), (0, end, c)]
-            else:
-                left_copy(c).wait_recv()
-                for g in range(2 * bounds[c], 2 * bounds[c + 1]):
+            held.append((k, c))
+            ready = [(k, c)] if c in lefts else []
+            if kind == "left":
+                left_copy(ce).wait_recv()
+                for g in range(2 * bounds[ce], 2 * bounds[ce + 1]):
                     tile = jnp.concatenate(
                         [left_r[g].astype(f32), jnp.zeros((LANES - cols, LANES), f32)], axis=0
                     )
                     left_e[g] = jnp.transpose(tile).astype(bf16)
-                todo = [(1, source, c), (0, source, c)]
+                lefts.append(ce)
+                ready += [(kk, cc) for kk, cc in held if cc == ce]
+            for kk, cc in ready:
+                far_block(z - sgn * kk, cc)
+            todo = [(source, c)]
+            if kind == "right":
+                todo.append((end, ce))
             for block in todo:
                 triangle_block(*block)
             queue.append(todo)
@@ -469,10 +488,9 @@
         def farther(k, carry):
             for c in range(chunks):
                 z_copy(z - sgn * k, c, 1 - inward).wait_recv()
-                for rowset in (1, 0):
-                    triangle_block(rowset, z - sgn * k, c)
-                for rowset in (1, 0):
-                    finish_block(rowset, z - sgn * k, c)
+                far_block(z - sgn * k, c)
+                triangle_block(z - sgn * k, c)
+                finish_block(z - sgn * k, c)
             return carry
 
         if nz > 4:
@@ -490,20 +508,20 @@
                         def _(source=source, direction=direction, c=c):
                             z_copy(source, c, direction).wait_recv()
                             z_copy(source, c, direction).start()
-                            triangle_block(0, source, c)
-                            finish_block(0, source, c)
+                            triangle_block(source, c)
+                            finish_block(source, c)
 
                 return carry
 
             lax.fori_loop(1, nz - 1, ring_step, 0)
             for c in range(chunks):
-                finish_block(0, z, c)
+                finish_block(z, c)
 
     @pl.when(is_end)
     def _():
         def arrived(source, c):
             z_copy(source, c, 1 - inward).wait_recv()
-            triangle_block(0, source, c)
+            triangle_block(source, c)
 
         def norm_if(here):
             if within:
@@ -511,29 +529,23 @@
                 @pl.when(here)
                 def _():
                     norm_turn(0)
-
-        for c in range(chunks):
-            arrived(near, c)
-        for c in range(chunks):
-            finish_block(0, z, c)
-        arrived(second, 0)
-        for c in range(chunks):
-            finish_block(0, near, c)
-        for c in range(1, chunks):
-            if c == chunks // 2:
-                norm_if(z // ratio == y)
-            arrived(second, c)
-            finish_block(0, second, c - 1)
-        finish_block(0, second, chunks - 1)
-        norm_if(z // ratio != y)
-        if within:
-            mix_turn(0)
 
         def farther_back(k, carry):
             for c in range(chunks):
                 return_block(near - sgn * k, c)
             return carry
 
+        for c in range(chunks):
+            arrived(near, c)
+        for c in range(chunks):
+            finish_block(z, c)
+        norm_if(z // ratio == y)
+        for c in range(chunks):
+            finish_block(near, c)
+        farther_back(1, 0)
+        norm_if(z // ratio != y)
+        if within:
+            mix_turn(0)
         lax.fori_loop(2, nz - 1, farther_back, 0)
 
     others = peaks.at[pl.ds(0, members - 1)]
@@ -552,28 +564,36 @@
         for sub in range(ratio):
             r = target * ratio + sub
 
-            @pl.when(jnp.logical_not(is_end) | (r == z) | (r == near) | (r == second))
+            @pl.when(jnp.logical_not(is_end) | (r == z) | (r == near))
             def _(sub=sub):
                 sent(send_t.at[0, target, sub], x_send.at[0, target, sub])
 
-            @pl.when(is_next & (r != end) & (r != z) & (r != near))
-            def _(sub=sub):
-                sent(send_t.at[1, target, sub], x_send.at[1, target, sub])
-
         return carry
 
     lax.fori_loop(1, ny, drain_x, 0)
+
+    def drain_far(r, carry):
+        @pl.when((r != end) & (r != z))
+        def _():
+            owner, sub = r // ratio, lax.rem(r, ratio)
+            sent(send_t.at[1, owner, sub], x_send.at[1, owner, sub])
+
+        return carry
+
+    @pl.when(is_next)
+    def _():
+        lax.fori_loop(0, nz, drain_far, 0)
 
     @pl.when(is_end)
     def _():
         sent(left_t, l_send)
 
     def drain_z(source, carry):
-        @pl.when((source <= z) & (z < nz - 1) & ((source >= z - 1) | (z <= nz - 3)))
+        @pl.when((source <= z) & (z < nz - 1) & ((source == z) | (z <= nz - 3)))
         def _():
             sent(right_all.at[source], z_send.at[0, source])
 
-        @pl.when((source >= z) & (z > 0) & ((source <= z + 1) | (z >= 2)))
+        @pl.when((source >= z) & (z > 0) & ((source == z) | (z >= 2)))
         def _():
             sent(right_all.at[source], z_send.at[1, source])
 
@@ -586,12 +606,7 @@
         mix_turn(turn)
 
     for sub in range(ratio):
-        r = y * ratio + sub
         sent(full_t.at[col, sub], c_send.at[sub])
-
-        @pl.when(is_next & (r != end) & (r != z) & (r != near))
-        def _(sub=sub):
-            sent(ret_t.at[sub], e_send.at[sub])
 
 
 def on_device(
@@ -642,10 +657,9 @@
             pltpu.VMEM((groups, cols, LANES), bf16),
             pltpu.VMEM((groups, LANES, LANES), bf16),
             pltpu.VMEM((nz, groups, cols, LANES), bf16),
-            pltpu.VMEM((2, ratio + 1, pairs) + tile, f32),
+            pltpu.VMEM((ratio + 1, pairs) + tile, f32),
             pltpu.VMEM((2, ny, ratio, pairs) + tile, bf16),
             pltpu.VMEM((2, ny, ratio, pairs) + tile, bf16),
-            pltpu.VMEM((ratio, pairs) + tile, bf16),
             pltpu.VMEM((2, ratio, pairs) + tile, bf16),
             pltpu.VMEM((ratio * rows * (channels + 1) + 8, LANES), f32),
             pltpu.VMEM((5, groups, LANES), f32),
@@ -660,8 +674,6 @@
             dma((chunks,)),
             dma((2, ny, ratio)),
             dma((2, ny, ratio, chunks)),
-            dma((ratio,)),
-            dma((ratio, chunks)),
             dma((ratio,)),
             dma((ratio, chunks)),
         ],

time: 39.4 us -> 38.5 us (0.977); the launches traced: 39.2 us -> 37.8 us
  Pallas kernels: 37.2 us -> 35.8 us
    pallas_call x1, Pallas kernels: 37.2 us -> 35.8 us  [on_device(): pl.pallas_call(functools.partial(kernel, (nz, ny, rows, cols, half, chunk...]
where the time goes in v6:
time: 38.5 us; the launch traced here: 37.8 us
  Pallas kernels  35.8 us (93%)
  local copies, waits for them, and re-layouts  1.4 us (4%)
  between operations  0.64 us (2%)
    pallas_call x1, Pallas kernels, on_device(): pl.pallas_call(functools.partial(kernel, (nz, ny, rows, cols, half, chunk...  35.8 us
    unnamed x2, local copies, waits for them, and re-layouts  1.4 us

profile of v6, /device:TPU:3, one launch (start us, length us, event | category | flops | bytes accessed | tf_op | source)
XLA Modules:
  0.0 37.8 jit_solution(10492315767027562779)
XLA Ops:
  0.6 35.8 %shard_map.113 = (bf16[40,64,80]{2,1,0:T(8,128)(2,1)S(1)}, f32[2,64]{1,0:T(2,128)S(1)}) custom-call(bf16[40,80,128]{2,1,0:T(8,128)(2,1)} %bitcast.13, s32[40,80]{1,0:T(8,128)} %bitcast.15, f32[2,64]{1,0:T(2,128)} %hist_smem.1, f32[2,64]{1,0:T(2,128)} %hist_smem.1, f32[1,128]{1,0:T(1,128)} %bitcast.18, f32[1,128]{1,0:T(1,128)} %bitcast.19, ...), custom_call_target="tpu_custom_call" | custom-call | tf_op jit(solution)/shard_map/pallas_call | solution.py:640
  36.4 0.8 %copy.14 = bf16[1,40,80,64]{2,3,1,0:T(8,128)(2,1)} copy(bf16[1,40,80,64]{2,3,1,0:T(8,128)(2,1)S(1)} %bitcast.12) | data formatting | bytes 819200
  37.3 0.6 %copy.15 = f32[2,64]{1,0:T(2,128)} copy(f32[2,64]{1,0:T(2,128)S(1)} %get-tuple-element.7) | data formatting | bytes 1024

commit v7 on v6

--- a/solution.py
+++ b/solution.py
@@ -542,11 +542,10 @@
         norm_if(z // ratio == y)
         for c in range(chunks):
             finish_block(near, c)
-        farther_back(1, 0)
+        lax.fori_loop(1, nz - 1, farther_back, 0)
         norm_if(z // ratio != y)
         if within:
             mix_turn(0)
-        lax.fori_loop(2, nz - 1, farther_back, 0)
 
     others = peaks.at[pl.ds(0, members - 1)]
     pltpu.make_async_copy(others, others, peak_recv).wait()

time: 38.5 us -> 37.8 us (0.982); the launches traced: 37.8 us -> 37.6 us
  no operation moved by 1% of the time
where the time goes in v7:
time: 37.8 us; the launch traced here: 37.6 us
  Pallas kernels  35.6 us (94%)
  local copies, waits for them, and re-layouts  1.4 us (4%)
  between operations  0.64 us (2%)
    pallas_call x1, Pallas kernels, on_device(): pl.pallas_call(functools.partial(kernel, (nz, ny, rows, cols, half, chunk...  35.6 us
    unnamed x2, local copies, waits for them, and re-layouts  1.4 us

profile of v7, /device:TPU:3, one launch (start us, length us, event | category | flops | bytes accessed | tf_op | source)
XLA Modules:
  0.0 37.6 jit_solution(4296333319934678241)
XLA Ops:
  0.6 35.6 %shard_map.113 = (bf16[40,64,80]{2,1,0:T(8,128)(2,1)S(1)}, f32[2,64]{1,0:T(2,128)S(1)}) custom-call(bf16[40,80,128]{2,1,0:T(8,128)(2,1)} %bitcast.13, s32[40,80]{1,0:T(8,128)} %bitcast.15, f32[2,64]{1,0:T(2,128)} %hist_smem.1, f32[2,64]{1,0:T(2,128)} %hist_smem.1, f32[1,128]{1,0:T(1,128)} %bitcast.18, f32[1,128]{1,0:T(1,128)} %bitcast.19, ...), custom_call_target="tpu_custom_call" | custom-call | tf_op jit(solution)/shard_map/pallas_call | solution.py:639
  36.2 0.8 %copy.14 = bf16[1,40,80,64]{2,3,1,0:T(8,128)(2,1)} copy(bf16[1,40,80,64]{2,3,1,0:T(8,128)(2,1)S(1)} %bitcast.12) | data formatting | bytes 819200
  37.1 0.6 %copy.15 = f32[2,64]{1,0:T(2,128)} copy(f32[2,64]{1,0:T(2,128)S(1)} %get-tuple-element.7) | data formatting | bytes 1024
